TPU v7x, 32 devices: a whole 2x2x4 slice. The times are simulated.
32 devices in a mesh: island: 4 (over z), fsdp: 8 (over y, x, core).
Axes of the slice: x: 2, y: 2, z: 4, core: 2. Of those that a mesh axis runs over, the one named last changes fastest.
Arguments:
- grads: bfloat16 [4, 1, 14336, 4096], P('island', None, 'fsdp'), may hold values from -200 to 200
- buffer: bfloat16 [4, 14336, 4096], P('island', 'fsdp'), may hold values from -200 to 200
- q_old: float32 [4, 4096, 128], P('island', 'fsdp'), may hold values from -0.09375 to 0.09375
- anchor: bfloat16 [14336, 4096], P('fsdp'), may hold values from -6 to 6
- momentum: float32 [14336, 4096], P(('fsdp', 'island')), may hold values from -6 to 6
Outputs:
- anchor_new: bfloat16 [14336, 4096], P('fsdp')
- buffer_new: bfloat16 [4, 14336, 4096], P('island', 'fsdp')
- momentum_new: float32 [14336, 4096], P(('fsdp', 'island'))
All inputs are finite; a program needn't handle non-finite values.
Results may differ from a plain program's by a relative error of at most 0.012.
Values may be sent and summed in bfloat16 or wider, within the bound.
No kernel may reach another device: no remote copies, remote signals or barrier semaphores. Data moves between devices by JAX's collectives and lax.ppermute only.
A program may use at most 192 MiB of HBM per device.

v0:
```python
import math

import jax
import jax.numpy as jnp
from jax import lax
from jax.sharding import PartitionSpec as P

ROWS = 14336
COLS = 4096
RANK = 128


precise = lax.Precision.HIGHEST
error_decay = 0.95
outer_beta = 0.9
outer_rate = 0.7
epsilon = 1e-06


def product(left_side, right_side, left_dims, right_dims):
    return lax.dot_general(
        left_side,
        right_side,
        (((left_dims,), (right_dims,)), ((), ())),
        precision=precise,
        preferred_element_type=jnp.float32,
    )


def inverse_upper(lower_factor):
    identity = jnp.eye(lower_factor.shape[0], dtype=lower_factor.dtype)
    return lax.linalg.triangular_solve(
        lower_factor, identity, left_side=True, lower=True, transpose_a=True
    )


def body(grads, buffer, q_old, anchor, momentum):
    rate = math.sqrt(ROWS * COLS / RANK)
    matrix = buffer[0].astype(jnp.float32) + grads[0, 0].astype(jnp.float32)
    raw_image = product(
        matrix,
        lax.all_gather(q_old[0].astype(jnp.bfloat16), "fsdp", axis=0, tiled=True).astype(
            jnp.float32
        ),
        1,
        0,
    )
    q_basis = None
    projected, gram_matrix = lax.psum(
        (product(matrix, raw_image, 0, 0), product(raw_image, raw_image, 0, 0)), "fsdp"
    )
    upper_inverse = inverse_upper(jnp.linalg.cholesky(gram_matrix))
    basis_rows = product(raw_image, upper_inverse, 1, 0)
    factor = product(projected, upper_inverse, 1, 0)
    q_basis = factor / jnp.sqrt(jnp.sum(factor * factor, axis=0) + epsilon)
    residue = matrix - (1.0 - error_decay) * product(basis_rows, factor, 1, 1)
    moved_sum = rate * product(basis_rows, q_basis, 1, 1)
    delta_total = lax.psum_scatter(
        moved_sum.astype(jnp.bfloat16), "island", scatter_dimension=0, tiled=True
    ).astype(jnp.float32)
    delta_mean = delta_total / lax.axis_size("island")
    momentum_new = outer_beta * momentum + delta_mean
    piece_rows = momentum.shape[0]
    anchor_piece = lax.dynamic_slice_in_dim(
        anchor, lax.axis_index("island") * piece_rows, piece_rows, 0
    ).astype(jnp.float32)
    anchor_share = (anchor_piece - outer_rate * (delta_mean + outer_beta * momentum_new)).astype(
        jnp.bfloat16
    )
    anchor_new = lax.all_gather(anchor_share, "island", axis=0, tiled=True)
    return (anchor_new, residue[None].astype(jnp.bfloat16), momentum_new)


def solution(mesh):
    in_specs = (
        P("island", None, "fsdp", None),
        P("island", "fsdp", None),
        P("island", "fsdp", None),
        P("fsdp", None),
        P(("fsdp", "island"), None),
    )
    out_specs = (P("fsdp", None), P("island", "fsdp", None), P(("fsdp", "island"), None))
    return jax.shard_map(body, mesh=mesh, in_specs=in_specs, out_specs=out_specs, check_vma=False)
```

profile of v0, /device:TPU:0, one launch (start us, length us, event | category | flops | bytes accessed | tf_op | source)
XLA Modules:
  0.0 754.1 jit_solution(14443960075709643727)
XLA Ops:
  7.2 0.0 all-gather.6.cloned.1.call-start
  7.2 1.6 convert_element_type.43
  8.8 0.0 all-gather.6.cloned.1.call-update
  8.9 0.0 all-reduce.3.cloned.1.call-start
  8.9 27.7 %all-gather.6.cloned.1.call-done = bf16[1,4096,128]{2,1,0:T(8,128)(2,1)} async-done(((bf16[1,512,128]{2,1,0:T(8,128)(2,1)}), bf16[1,4096,128]{2,1,0:T(8,128)(2,1)}) %all-gather.6.cloned.1.call-update) | async-done | bytes 1048592 | tf_op jit(solution)/shard_map/all_gather | solution.py:42
  36.6 19.1 %fusion.1 = f32[1792,128]{1,0:T(8,128)S(1)} fusion(bf16[1,1,1792,4096]{3,2,1,0:T(8,128)(2,1)} %param.5, bf16[1,1792,4096]{2,1,0:T(8,128)(2,1)} %param.6, bf16[1,4096,128]{2,1,0:T(8,128)(2,1)} %all-gather.6.cloned.1.call-done), kind=kOutput, calls=%fused_computation.4 | convolution fusion | flops 11296309248 | bytes 31326208 | tf_op jit(solution)/shard_map/dot_general | solution.py:21
  55.7 2.2 fusion.14
  57.9 50.6 %fusion = f32[4096,128]{1,0:T(8,128)} fusion(f32[1792,128]{1,0:T(8,128)S(1)} %fusion.1, bf16[1,1,1792,4096]{3,2,1,0:T(8,128)(2,1)} %param.5, bf16[1,1792,4096]{2,1,0:T(8,128)(2,1)} %param.6), kind=kOutput, calls=%fused_computation.3 | convolution fusion | flops 11296309248 | bytes 32374784 | tf_op jit(solution)/shard_map/dot_general | solution.py:21
  108.5 0.0 all-reduce.3.cloned.1.call-update
  108.6 0.6 reduce-scatter.2.cloned.1.call-start
  109.1 61.9 %all-reduce.3.cloned.1.call-done = (f32[128,128]{0,1:T(8,128)}, f32[4096,128]{1,0:T(8,128)}) async-done(((f32[128,128]{0,1:T(8,128)}, f32[4096,128]{1,0:T(8,128)}), (f32[128,128]{0,1:T(8,128)}, f32[4096,128]{1,0:T(8,128)})) %all-reduce.3.cloned.1.call-update) | async-done | bytes 2162704 | tf_op jit(solution)/shard_map/psum | solution.py:49
  171.0 0.9 copy.9
  171.9 0.9 fusion.13
  172.8 11.7 %cholesky.17 = f32[128,128]{1,0:T(8,128)S(1)} custom-call(f32[128,128]{1,0:T(8,128)S(1)} %fusion.13), custom_call_target="Cholesky" | custom-call | tf_op jit(solution)/shard_map/jit(cholesky)/cholesky | solution.py:52
  184.5 0.6 compare_reduce_fusion
  185.2 0.7 fusion.10
  185.8 9.8 %custom-call.6 = f32[1,128,128]{1,2,0:T(8,128)S(1)} custom-call(f32[1,128,128]{2,1,0:T(8,128)S(1)} %fusion.10), custom_call_target="InvertDiagBlocksLowerTriangular" | custom-call | tf_op jit(solution)/shard_map/triangular_solve | solution.py:32
  195.7 0.2 fusion.11
  195.9 0.9 fusion.15
  196.7 3.4 multiply_reduce_fusion
  200.1 26.1 %multiply_convert_fusion = bf16[1792,4096]{1,0:T(8,128)(2,1)} fusion(f32[1792,128]{1,0:T(8,128)S(1)} %fusion.15, f32[4096,128]{1,0:T(8,128)S(1)} %get-tuple-element.8, f32[128]{0:T(128)S(1)} %add_sqrt_fusion), kind=kOutput, calls=%fused_computation.2 | convolution fusion | flops 11289493504 | bytes 17695232 | tf_op jit(solution)/shard_map/dot_general | solution.py:21
  226.3 0.0 reduce-scatter.2.cloned.1.call-update
  226.3 0.0 all-gather.4.cloned.1.call-start
  226.3 244.9 %reduce-scatter.2.cloned.1.call-done = bf16[448,4096]{1,0:T(8,128)(2,1)} async-done(((bf16[1792,4096]{1,0:T(8,128)(2,1)}), bf16[448,4096]{1,0:T(8,128)(2,1)}) %reduce-scatter.2.cloned.1.call-update) | async-done | bytes 3670032 | tf_op jit(solution)/shard_map/reduce_scatter | solution.py:58
  471.3 9.0 %subtract_convert_fusion.1 = (bf16[448,4096]{1,0:T(8,128)(2,1)}, f32[448,4096]{1,0:T(8,128)}) fusion(bf16[448,4096]{1,0:T(8,128)(2,1)} %reduce-scatter.2.cloned.1.call-done, bf16[1792,4096]{1,0:T(8,128)(2,1)} %param.8, s32[]{:T(128)S(6)} %select_n.7, f32[448,4096]{1,0:T(8,128)} %param.9), kind=kLoop, calls=%fused_computation.10 | loop fusion | flops 18350080 | bytes 25690116 | tf_op jit(solution)/shard_map/convert_element_type | solution.py:67
  480.3 0.0 all-gather.4.cloned.1.call-update
  480.3 32.3 %fusion.6 = bf16[1,1792,4096]{2,1,0:T(8,128)(2,1)} fusion(f32[1792,128]{1,0:T(8,128)S(1)} %fusion.15, f32[4096,128]{1,0:T(8,128)S(1)} %get-tuple-element.8, bf16[1,1,1792,4096]{3,2,1,0:T(8,128)(2,1)} %param.5, bf16[1,1792,4096]{2,1,0:T(8,128)(2,1)} %param.6), kind=kOutput, calls=%fused_computation.9 | convolution fusion | flops 11318329344 | bytes 47054848 | tf_op jit(solution)/shard_map/dot_general | solution.py:21
  512.6 221.4 %all-gather.4.cloned.1.call-done = bf16[1792,4096]{1,0:T(8,128)(2,1)} async-done(((bf16[448,4096]{1,0:T(8,128)(2,1)}), bf16[1792,4096]{1,0:T(8,128)(2,1)}) %all-gather.4.cloned.1.call-update) | async-done | bytes 14680080 | tf_op jit(solution)/shard_map/all_gather | solution.py:70
  733.9 13.4 %copy.14 = bf16[1792,4096]{1,0:T(8,128)(2,1)} copy(bf16[1792,4096]{1,0:T(8,128)(2,1)} %all-gather.4.cloned.1.call-done) | data formatting | bytes 29360128
  (2 shorter events, 0.0 us)
Async XLA Ops:
  7.2 29.4 %all-gather.6.cloned.1.call-start = ((), (), s32[]{:S(2)}) async-start(), calls=%async_computation.3 | async-start | bytes 1179648 | tf_op jit(solution)/shard_map/all_gather | solution.py:42
  8.9 162.1 %all-reduce.3.cloned.1.call-start = ((), (), s32[]{:S(2)}) async-start(), calls=%async_computation.4 | async-start | bytes 4325376 | tf_op jit(solution)/shard_map/psum | solution.py:49
  108.6 362.7 %reduce-scatter.2.cloned.1.call-start = ((), (), s32[]{:S(2)}) async-start(), calls=%async_computation.1 | async-start | bytes 18350080 | tf_op jit(solution)/shard_map/reduce_scatter | solution.py:58
  226.3 507.6 %all-gather.4.cloned.1.call-start = ((), (), s32[]{:S(2)}) async-start(), calls=%async_computation.2 | async-start | bytes 18350080 | tf_op jit(solution)/shard_map/all_gather | solution.py:70
Sparse Core Ops, SparseCore 0:
  10.4 26.0 all-gather.5
  108.7 62.2 all-reduce.2
  226.4 244.8 reduce-scatter.1
  480.4 253.4 all-gather.3
where the time goes:
time: 759 us; the launch traced here: 754 us
  waiting for transfers between devices  556 us (73%)
  matrix products  135 us (18%)
  other arithmetic  34.3 us (5%)
  local copies, waits for them, and re-layouts  14.3 us (2%)
  between operations  14.1 us (2%)
    reduce_scatter x1, waiting for transfers between devices, body(): lax.psum_scatter(moved_sum.astype(jnp.bfloat16), 'island', scatter_dimens...  245 us
    all_gather x1, waiting for transfers between devices, body(): anchor_new = lax.all_gather(anchor_share, 'island', axis=0, tiled=True)  221 us
    dot_general x7, matrix products, product(): lax.dot_general(left_side, right_side, (((left_dims,), (right_dims,)), ((...  135 us
    psum x1, waiting for transfers between devices, body(): lax.psum((product(matrix, raw_image, 0, 0), product(raw_image, raw_image,...  61.9 us
    all_gather x1, waiting for transfers between devices, body(): lax.all_gather(q_old[0].astype(jnp.bfloat16), 'fsdp', axis=0, tiled=True)  27.7 us
  transfers between devices with their start and end apart: 4, of which 4 were waited for; matrix products, arithmetic and copies ran while one was open for 4% of the time, Pallas kernels for 0%

commit v1 on v0

v1 whole, which is shorter than its diff:
```python
import functools
import math

import jax
import jax.numpy as jnp
from jax import lax
from jax.experimental import pallas as pl
from jax.experimental.pallas import tpu as pltpu
from jax.sharding import PartitionSpec as P


precise = lax.Precision.HIGHEST
error_decay = 0.95
outer_beta = 0.9
outer_rate = 0.7
epsilon = 1e-06
bf16 = jnp.bfloat16
f32 = jnp.float32


def params(mib):
    return pltpu.CompilerParams(
        dimension_semantics=("arbitrary",), vmem_limit_bytes=mib * 1024 * 1024
    )


def cost(flops, moved):
    return pl.CostEstimate(flops=int(flops), bytes_accessed=int(moved), transcendentals=0)


def divisor(total, most, step):
    return max(d for d in range(step, most + 1, step) if total % d == 0)


def project_kernel(slots, g_ref, b_ref, q_ref, raw_ref, proj_ref, gram_ref, q_scratch):
    blocks, width, _ = q_ref.shape

    @pl.when(pl.program_id(0) == 0)
    def _():
        proj_ref[...] = jnp.zeros_like(proj_ref)
        gram_ref[...] = jnp.zeros_like(gram_ref)
        for j in range(blocks):
            q_scratch[j * width : (j + 1) * width, :] = q_ref[slots[j]]

    matrix = g_ref[...] + b_ref[...]
    raw = jnp.dot(matrix, q_scratch[...], preferred_element_type=f32)
    raw_ref[...] = raw
    turned = raw.T
    gram_ref[...] += jnp.dot(turned, raw, precision=precise, preferred_element_type=f32)
    turned = turned.astype(bf16)
    for j in range(blocks):
        proj_ref[slots[j]] += jnp.dot(
            turned, matrix[:, j * width : (j + 1) * width], preferred_element_type=f32
        )


def project(slots, grads, buffer, q_stack):
    rows, cols = grads.shape
    blocks, width, rank = q_stack.shape
    step = divisor(rows, 256, 8)
    tile = pl.BlockSpec((step, cols), lambda i, s: (i, 0))
    whole = lambda shape: pl.BlockSpec(shape, lambda i, s: (0,) * len(shape))
    return pl.pallas_call(
        project_kernel,
        grid_spec=pltpu.PrefetchScalarGridSpec(
            num_scalar_prefetch=1,
            grid=(rows // step,),
            in_specs=[tile, tile, whole((blocks, width, rank))],
            out_specs=[
                pl.BlockSpec((step, rank), lambda i, s: (i, 0)),
                whole((blocks, rank, width)),
                whole((rank, rank)),
            ],
            scratch_shapes=[pltpu.VMEM((cols, rank), bf16)],
        ),
        out_shape=[
            jax.ShapeDtypeStruct((rows, rank), f32),
            jax.ShapeDtypeStruct((blocks, rank, width), f32),
            jax.ShapeDtypeStruct((rank, rank), f32),
        ],
        compiler_params=params(48),
        cost_estimate=cost(4 * rows * cols * rank, 4 * rows * cols),
        name="project",
    )(slots, grads, buffer, q_stack)


def residue_kernel(slots, g_ref, b_ref, p_ref, r_ref, out_ref):
    blocks, _, width = r_ref.shape
    basis = p_ref[...]
    for j in range(blocks):
        at = slice(j * width, (j + 1) * width)
        update = jnp.dot(basis, r_ref[slots[j]], preferred_element_type=f32)
        matrix = g_ref[:, at].astype(f32) + b_ref[:, at].astype(f32)
        out_ref[:, at] = (matrix - (1.0 - error_decay) * update).astype(bf16)


def residue(slots, grads, buffer, basis, stack):
    rows, cols = grads.shape
    blocks, _, width = stack.shape
    rank = basis.shape[1]
    step = divisor(rows, 256, 8)
    tile = pl.BlockSpec((step, cols), lambda i, s: (i, 0))
    return pl.pallas_call(
        residue_kernel,
        grid_spec=pltpu.PrefetchScalarGridSpec(
            num_scalar_prefetch=1,
            grid=(rows // step,),
            in_specs=[
                tile,
                tile,
                pl.BlockSpec((step, rank), lambda i, s: (i, 0)),
                pl.BlockSpec((blocks, rank, width), lambda i, s: (0, 0, 0)),
            ],
            out_specs=tile,
        ),
        out_shape=jax.ShapeDtypeStruct((rows, cols), bf16),
        compiler_params=params(48),
        cost_estimate=cost(2 * rows * cols * rank, 6 * rows * cols),
        name="residue",
    )(slots, grads, buffer, basis, stack)


def outer(momentum, anchor, mean):
    momentum_new = outer_beta * momentum + mean
    anchor_new = anchor.astype(f32) - outer_rate * (mean + outer_beta * momentum_new)
    return momentum_new, anchor_new.astype(bf16)


def scaled(rows, scale):
    return (rows.astype(f32) * scale).astype(bf16)


def change(left, low_ref, high_ref):
    depth = low_ref.shape[1]
    return jnp.dot(left[:, :depth], low_ref[0], preferred_element_type=f32) + jnp.dot(
        left[:, depth:], high_ref[0], preferred_element_type=f32
    )


def late_kernel(n, scalars, *refs):
    p_refs, (scale, low, high, m_ref, a_ref), refs = refs[:n], refs[n : n + 5], refs[n + 5 :]
    m_out, a_out, share, left = refs[-4:]
    rank = p_refs[0].shape[-1]

    @pl.when(pl.program_id(0) == 0)
    def _():
        for d in range(n):
            at = slice(d * rank, (d + 1) * rank)
            left[:, at] = scaled(p_refs[d][0, 0] if d == 0 else p_refs[d][0], scale[:, at])

    momentum_new, anchor_new = outer(m_ref[0], a_ref[0, 0], change(left, low, high))
    m_out[0] = momentum_new
    a_out[0, 0] = anchor_new
    share[...] = anchor_new


def stack_specs(stacks, start):
    blocks = stacks[0].shape[0]
    return [
        pl.BlockSpec(
            (1, *stack.shape[1:]), lambda j, s, k=k: (s[1 + k * blocks + start + j], 0, 0)
        )
        for k, stack in enumerate(stacks)
    ]


def late(scalars, own, others, scale, stacks, momentum, anchor, span, filled):
    n, parts, height, _ = anchor.shape
    width, depth, rank = stacks[0].shape[-1], scale.shape[-1], own.shape[-1]
    last, (start, stop) = parts - 1, span
    fixed = lambda *at: (lambda j, s: at)
    m_spec = pl.BlockSpec((1, height, width), lambda j, s: (last, 0, start + j))
    a_spec = pl.BlockSpec((1, 1, height, width), lambda j, s: (s[0], last, 0, start + j))
    columns = (stop - start) * width
    return pl.pallas_call(
        functools.partial(late_kernel, n),
        grid_spec=pltpu.PrefetchScalarGridSpec(
            num_scalar_prefetch=1,
            grid=(stop - start,),
            in_specs=[pl.BlockSpec((1, 1, height, rank), lambda j, s: (s[0], last, 0, 0))]
            + [pl.BlockSpec((1, height, rank), fixed(last * n, 0, 0))] * (n - 1)
            + [pl.BlockSpec((1, depth), fixed(0, 0)), *stack_specs(stacks, start), m_spec, a_spec]
            + [pl.BlockSpec(memory_space=pl.ANY)] * len(filled),
            out_specs=[m_spec, a_spec, pl.BlockSpec((height, width), lambda j, s: (0, j))],
            scratch_shapes=[pltpu.VMEM((height, depth), bf16)],
        ),
        out_shape=[
            jax.ShapeDtypeStruct(momentum.shape, f32),
            jax.ShapeDtypeStruct(anchor.shape, bf16),
            jax.ShapeDtypeStruct((height, columns), bf16),
        ],
        input_output_aliases={n + 6 + k: k for k in range(len(filled))},
        compiler_params=params(48),
        cost_estimate=cost(2 * height * columns * depth, 14 * height * columns),
        name="late",
    )(scalars, own, *others, scale, *stacks, momentum, anchor, *filled)


def early_kernel(n, counts, scalars, *refs):
    p_refs, refs = refs[:n], refs[n:]
    (scale, low, high, m_ref, a_ref), refs = refs[:5], refs[5:]
    got, refs = refs[: sum(counts)], refs[sum(counts) :]
    _, _, m_out, a_out, left, mean = refs
    rank, height = p_refs[0].shape[-1], p_refs[0].shape[-2]

    @pl.when(pl.program_id(0) == 0)
    def _():
        for d in range(n):
            at = slice(d * rank, (d + 1) * rank)
            for k in range(n):
                rows = p_refs[d][k, 0] if d == 0 else p_refs[d][k]
                left[k * height : (k + 1) * height, at] = scaled(rows, scale[:, at])

    mean[...] = change(left, low, high).reshape(mean.shape)
    for d in range(n):
        k = lax.rem(scalars[0] + d, n)
        if d == 0:
            momentum = m_ref[0]
        else:
            start = sum(counts[: d - 1])
            momentum = got[start][...].astype(f32)
            for ref in got[start + 1 : start + counts[d - 1]]:
                momentum = momentum + ref[...].astype(f32)
        momentum_new, anchor_new = outer(momentum, a_ref[k, 0], mean[k])
        if d == 0:
            m_out[0] = momentum_new
        a_out[k, 0] = anchor_new


def early(scalars, own, others, scale, stacks, momentum, anchor, got, filled):
    n, _, height, cols = anchor.shape
    blocks, _, width = stacks[0].shape
    depth, rank = scale.shape[-1], own.shape[-1]
    counts = [len(pieces) for pieces in got]
    flat = [piece for pieces in got for piece in pieces]
    fixed = lambda *at: (lambda j, s: at)
    m_spec = pl.BlockSpec((1, height, width), lambda j, s: (0, 0, j))
    a_spec = pl.BlockSpec((n, 1, height, width), lambda j, s: (0, 0, 0, j))
    first_alias = n + 6 + len(flat)
    return pl.pallas_call(
        functools.partial(early_kernel, n, counts),
        grid_spec=pltpu.PrefetchScalarGridSpec(
            num_scalar_prefetch=1,
            grid=(blocks,),
            in_specs=[pl.BlockSpec((n, 1, height, rank), fixed(0, 0, 0, 0))]
            + [pl.BlockSpec((n, height, rank), fixed(0, 0, 0))] * (n - 1)
            + [pl.BlockSpec((1, depth), fixed(0, 0)), *stack_specs(stacks, 0), m_spec, a_spec]
            + [pl.BlockSpec((height, width), lambda j, s: (0, j))] * len(flat)
            + [pl.BlockSpec(memory_space=pl.ANY)] * 2,
            out_specs=[m_spec, a_spec],
            scratch_shapes=[
                pltpu.VMEM((n * height, depth), bf16),
                pltpu.VMEM((n, height, width), f32),
            ],
        ),
        out_shape=[
            jax.ShapeDtypeStruct(momentum.shape, f32),
            jax.ShapeDtypeStruct(anchor.shape, bf16),
        ],
        input_output_aliases={first_alias: 0, first_alias + 1: 1},
        compiler_params=params(56),
        cost_estimate=cost(2 * n * height * cols * depth, 32 * height * cols),
        name="early",
    )(scalars, own, *others, scale, *stacks, momentum, anchor, *flat, *filled)


def swap(x, bit):
    size = lax.axis_size("fsdp")
    return lax.ppermute(x, "fsdp", [(i, i ^ bit) for i in range(size)])


def spread(x, bits):
    for bit in bits:
        x = jnp.concatenate([x, swap(x, bit)], axis=0)
    return x


def places(apart, bits):
    return functools.reduce(
        jnp.bitwise_or,
        [((apart >> bit.bit_length() - 1) & 1) << k for k, bit in enumerate(bits)],
        jnp.zeros_like(apart),
    )


def from_island(x, ahead):
    n = lax.axis_size("island")
    return lax.ppermute(x, "island", [(s, (s - ahead) % n) for s in range(n)])


def near(x):
    return from_island(x, 1), from_island(x, lax.axis_size("island") - 1)


def onward(above, below):
    down = lax.ppermute(above, "island", [(1, 0), (2, 1)])
    up = lax.ppermute(below, "island", [(1, 2), (2, 3)])
    return down, up


def line_step(down, up, step):
    n = lax.axis_size("island")
    down = lax.ppermute(down, "island", [(k, k - 1) for k in range(1, n - step + 1)])
    up = lax.ppermute(up, "island", [(k, k + 1) for k in range(step - 1, n - 1)])
    return down, up


def tie(*values):
    return lax.optimization_barrier(values)


def exact(a, b):
    return jnp.dot(a, b, precision=precise, preferred_element_type=f32)


def body(grads, buffer, q_old, anchor, momentum):
    n, size = lax.axis_size("island"), lax.axis_size("fsdp")
    island, place = lax.axis_index("island"), lax.axis_index("fsdp")
    grads, buffer, q_old = grads[0, 0], buffer[0], q_old[0]
    rows, cols = grads.shape
    rank = q_old.shape[1]
    rate = math.sqrt(rows * size * cols / rank)

    quarter = momentum.shape[0]
    parts = 2 if quarter % 16 == 0 else 1
    height = quarter // parts
    momentum = momentum.reshape(parts, height, cols)
    anchor = anchor.reshape(n, parts, height, cols)
    forward = n == 4
    if parts == 2:
        ahead = momentum[0].astype(bf16)
        got = near(ahead) if forward else [from_island(ahead, d) for d in range(1, n)]

    bits = [1 << k for k in range(size.bit_length() - 1)]
    split = size == 1 << len(bits) and (cols // size) % 128 == 0
    q_own = q_old.astype(bf16)
    if split:
        falling = bits[::-1]
        crossed = falling[1::-1] + falling[2:]
        q_stack = spread(q_own[None], falling)
        apart = jnp.arange(size) ^ place
        slots, others_slots = places(apart, falling), places(apart, crossed)
    else:
        width = 512 if cols % 512 == 0 else cols
        slots = others_slots = jnp.arange(cols // width)
        q_stack = lax.all_gather(q_own, "fsdp", axis=0, tiled=True).reshape(-1, width, rank)
    scalars = jnp.concatenate([island[None], slots, others_slots]).astype(jnp.int32)
    slots = slots.astype(jnp.int32)
    blocks = slots.shape[0]

    raw, projected, gram = project(slots, grads, buffer, q_stack)
    if split:
        for bit in bits:
            gram = gram + swap(gram, bit)
        for bit in bits:
            half = projected.shape[0] // 2
            projected = projected[:half] + swap(projected[half:], bit)
    else:
        projected, gram = lax.psum((projected, gram), "fsdp")
    lower = jnp.linalg.cholesky(gram)
    upper_inverse = lax.linalg.triangular_solve(
        lower, jnp.eye(rank, dtype=f32), left_side=True, lower=True, transpose_a=True
    )
    factor = jnp.einsum(
        "kr,bkw->brw", upper_inverse, projected, precision=precise, preferred_element_type=f32
    ).astype(bf16)
    pieces = [from_island(factor, d) for d in range(1, n)]
    pieces = [factor, *pieces]

    basis = exact(raw, upper_inverse).astype(bf16)
    by_part = basis.reshape(n, parts, height, rank)
    others = []
    for d in range(1, n):
        wanted = lax.dynamic_index_in_dim(by_part[:, -1], (island + n - d) % n, 0)
        sent = jnp.concatenate([by_part[:, 0], wanted], 0) if parts == 2 else wanted
        others.append(from_island(sent, d))

    if parts == 2 and forward:
        above, below = got
        down, up = onward(above, below)
        got = [(above,), (down, up), (below,)]
    elif parts == 2:
        got = [(piece,) for piece in got]
    stacks = [jnp.concatenate(pieces[:2], axis=1), jnp.concatenate(pieces[2:], axis=1)]
    if split:
        for pair in zip(falling, crossed):
            stacks = [spread(x, [bit]) for x, bit in zip(stacks, pair)]
    squares = [jnp.sum(jnp.square(x.astype(f32)), axis=(0, 2)) for x in stacks]
    scale = ((rate / n) / jnp.sqrt(jnp.concatenate(squares) + epsilon))[None]

    first, filled = [], []
    count = 2 if forward and blocks % 2 == 0 else 1
    for k in range(count):
        span = (k * blocks // count, (k + 1) * blocks // count)
        *filled, share = late(
            scalars, by_part, others, scale, stacks, momentum, anchor, span, filled
        )
        if forward:
            first.append(line_step(share, share, 1))
    low, *_ = tie(stacks[0], share)
    buffer_new = residue(slots, grads, buffer, basis, low)
    found = {}
    if forward:
        (*flat, buffer_new) = tie(*first[0], buffer_new)
        second = [line_step(*flat, 2)]
    if parts == 2:
        filled = early(
            scalars, by_part, others, scale, stacks, momentum, anchor, got, filled
        )
    momentum_new, anchor_new = filled
    if forward:
        if count == 2:
            (*flat, anchor_new) = tie(*first[1], anchor_new)
            second.append(line_step(*flat, 2))
        third = []
        for pair in second:
            third.append(line_step(*pair, 3))
        for d, (down, up) in ((1, (first, third)), (2, (second, second)), (3, (third, first))):
            found[d] = [x[0] + y[1] for x, y in zip(down, up)]
    else:
        found = {d: [from_island(share, d)] for d in range(1, n)}
    for k in range(count):
        for d in found:
            anchor_new = lax.dynamic_update_slice(
                anchor_new,
                found[d][k][None, None],
                ((island + d) % n, parts - 1, 0, k * cols // count),
            )
    return (
        anchor_new.reshape(rows, cols),
        buffer_new[None],
        momentum_new.reshape(quarter, cols),
    )


def solution(mesh):
    in_specs = (
        P("island", None, "fsdp", None),
        P("island", "fsdp", None),
        P("island", "fsdp", None),
        P("fsdp", None),
        P(("fsdp", "island"), None),
    )
    out_specs = (P("fsdp", None), P("island", "fsdp", None), P(("fsdp", "island"), None))

    return jax.shard_map(body, mesh=mesh, in_specs=in_specs, out_specs=out_specs, check_vma=False)
```

time: 759 us -> 387 us (0.51)
  waiting for transfers between devices: 556 us -> 220 us
  matrix products: 135 us -> 1.46 us
  Pallas kernels: 0 us -> 62.1 us
  starting transfers between devices: 0.69 us -> 52.5 us
  between operations: 14.1 us -> 1.13 us
  other arithmetic: 34.3 us -> 42.5 us
    all_gather x2 -> x0, waiting for transfers between devices: 249 us -> none  [the longest x1 221 us: body(): anchor_new = lax.all_gather(anchor_share, 'island', axis=0, tiled=True)]
    reduce_scatter x1 -> x0, waiting for transfers between devices: 245 us -> none  [body(): lax.psum_scatter(moved_sum.astype(jnp.bfloat16), 'island', scatter_dimens...]
    ppermute x0 -> x37, waiting for transfers between devices: none -> 220 us  [the longest x6 101 us: line_step(): lax.ppermute(down, 'island', [(k, k - 1) for k in range(1, n - step + 1)])]
    dot_general x7 -> x2, matrix products: 135 us -> 1.28 us  [the longest x1 0.87 us: exact(): return jnp.dot(a, b, precision=precise, preferred_element_type=f32)]
    pallas_call x0 -> x5, Pallas kernels: none -> 62.1 us  [the longest x1 19.2 us: residue(): pl.pallas_call(residue_kernel, grid_spec=pltpu.PrefetchScalarGridSpec(num...]
    psum x1 -> x0, waiting for transfers between devices: 61.9 us -> none  [body(): lax.psum((product(matrix, raw_image, 0, 0), product(raw_image, raw_image,...]
    ppermute x0 -> x37, starting transfers between devices: none -> 52.5 us  [the longest x8 15 us: from_island(): return lax.ppermute(x, 'island', [(s, (s - ahead) % n) for s in range(n)])]
    unnamed x1 -> x19, local copies, waits for them, and re-layouts: 13.4 us -> 2.23 us
  transfers between devices with their start and end apart: 4 -> 37, of which waited for: 4 -> 19; matrix products, arithmetic and copies ran while one was open for 4% -> 11% of each run, Pallas kernels for 0% -> 12%
where the time goes in v1:
time: 387 us; the launch traced here: 386 us
  waiting for transfers between devices  220 us (57%)
  Pallas kernels  62.1 us (16%)
  starting transfers between devices  52.5 us (14%)
  other arithmetic  42.5 us (11%)
  local copies, waits for them, and re-layouts  7.07 us (2%)
    ppermute x6, waiting for transfers between devices, line_step(): lax.ppermute(down, 'island', [(k, k - 1) for k in range(1, n - step + 1)])  101 us
    ppermute x8, waiting for transfers between devices, from_island(): return lax.ppermute(x, 'island', [(s, (s - ahead) % n) for s in range(n)])  85.7 us
    ppermute x15, waiting for transfers between devices, swap(): return lax.ppermute(x, 'fsdp', [(i, i ^ bit) for i in range(size)])  23.5 us
    pallas_call x1, Pallas kernels, residue(): pl.pallas_call(residue_kernel, grid_spec=pltpu.PrefetchScalarGridSpec(num...  19.2 us
    pallas_call x1, Pallas kernels, early(): pl.pallas_call(functools.partial(early_kernel, n, counts), grid_spec=pltp...  17.2 us
    ppermute x8, starting transfers between devices, from_island(): return lax.ppermute(x, 'island', [(s, (s - ahead) % n) for s in range(n)])  15 us
    pallas_call x1, Pallas kernels, project(): pl.pallas_call(project_kernel, grid_spec=pltpu.PrefetchScalarGridSpec(num...  14.9 us
    ppermute x15, starting transfers between devices, swap(): return lax.ppermute(x, 'fsdp', [(i, i ^ bit) for i in range(size)])  14.7 us
  transfers between devices with their start and end apart: 37, of which 19 were waited for; matrix products, arithmetic and copies ran while one was open for 11% of the time, Pallas kernels for 12%

profile of v1, /device:TPU:0, one launch (start us, length us, event | category | flops | bytes accessed | tf_op | source)
XLA Modules:
  0.0 386.4 jit_solution(16067379817660160558)
XLA Ops:
  1.6 3.1 collective-permute-start
  4.7 3.5 collective-permute-done
  8.2 1.8 collective-permute-start.1
  10.0 5.8 %collective-permute-done.1 = bf16[2,512,128]{2,1,0:T(8,128)(2,1)S(1)} collective-permute-done((bf16[2,512,128]{2,1,0:T(8,128)(2,1)S(1)}, bf16[2,512,128]{2,1,0:T(8,128)(2,1)S(1)}, u32[]{:S(2)}, u32[]{:S(2)}) %collective-permute-start.1) | collective-permute-done | bytes 262176 | tf_op jit(solution)/shard_map/ppermute | solution.py:269
  15.9 1.9 collective-permute-done.2
  17.9 14.9 %project.1 = (f32[1792,128]{1,0:T(8,128)S(1)}, f32[8,128,512]{2,1,0:T(8,128)S(1)}, f32[128,128]{1,0:T(8,128)S(1)}) custom-call(s32[8]{0:T(128)S(1)} %or_or_fusion.1.slots, bf16[1792,4096]{1,0:T(8,128)(2,1)} %bitcast.62, bf16[1792,4096]{1,0:T(8,128)(2,1)} %bitcast.64, bf16[8,512,128]{2,1,0:T(8,128)(2,1)S(1)} %pad_maximum_fusion.2.q_ref), custom_call_target="tpu_custom_call" | custom-call | flops 3758096384 | bytes 29360128 | tf_op jit(solution)/shard_map/project/pallas_call | solution.py:63
  34.5 2.3 collective-permute-done.3
  36.9 1.5 collective-permute-start.4
  38.4 1.5 slice_add_fusion
  41.5 1.5 collective-permute-start.5
  43.0 2.8 collective-permute-done.5
  46.0 11.7 %cholesky.17 = f32[128,128]{1,0:T(8,128)S(1)} custom-call(f32[128,128]{1,0:T(8,128)S(1)} %fusion.6), custom_call_target="Cholesky" | custom-call | tf_op jit(solution)/shard_map/jit(cholesky)/cholesky | solution.py:360
  59.5 1.5 collective-permute-start.11
  61.7 9.8 %custom-call.6 = f32[1,128,128]{1,2,0:T(8,128)S(1)} custom-call(f32[1,128,128]{2,1,0:T(8,128)S(1)} %fusion.3), custom_call_target="InvertDiagBlocksLowerTriangular" | custom-call | tf_op jit(solution)/shard_map/triangular_solve | solution.py:361
  72.1 3.7 collective-permute-start.12
  75.8 3.9 %collective-permute-done.12 = bf16[1,128,512]{2,1,0:T(8,128)(2,1)S(1)} collective-permute-done((bf16[1,128,512]{2,1,0:T(8,128)(2,1)S(1)}, bf16[1,128,512]{2,1,0:T(8,128)(2,1)S(1)}, u32[]{:S(2)}, u32[]{:S(2)}) %collective-permute-start.12) | collective-permute-done | bytes 131104 | tf_op jit(solution)/shard_map/ppermute | solution.py:288
  79.9 4.6 %collective-permute-start.17 = (bf16[1,128,512]{2,1,0:T(8,128)(2,1)S(1)}, bf16[1,128,512]{2,1,0:T(8,128)(2,1)S(1)}, u32[]{:S(2)}, u32[]{:S(2)}) collective-permute-start(bf16[1,128,512]{2,1,0:T(8,128)(2,1)S(1)} %fusion), channel_id=1, source_target_pairs={{0,8},{8,16},{16,24},{24,0},{1,9},{9,17},{17,25},{25,1},{2,10},{10... | collective-permute-start | bytes 393224 | tf_op jit(solution)/shard_map/ppermute | solution.py:288
  84.8 2.3 collective-permute-done.17
  87.1 1.9 collective-permute-start.18
  89.3 3.5 slice.67
  92.8 2.8 collective-permute-start.23
  97.2 1.7 collective-permute-start.19
  98.9 4.3 %collective-permute-done.14 = bf16[2,256,512]{2,1,0:T(8,128)(2,1)S(1)} collective-permute-done((bf16[2,256,512]{2,1,0:T(8,128)(2,1)S(1)}, bf16[2,256,512]{2,1,0:T(8,128)(2,1)S(1)}, u32[]{:S(2)}, u32[]{:S(2)}) %collective-permute-start.14) | collective-permute-done | bytes 524320 | tf_op jit(solution)/shard_map/ppermute | solution.py:269
  104.2 2.4 collective-permute-done.19
  108.8 2.4 collective-permute-start.8
  111.2 1.3 collective-permute-start.7
  112.5 1.9 multiply_reduce_fusion.1
  114.4 69.1 %collective-permute-done.23.refs_9_ = bf16[224,4096]{1,0:T(8,128)(2,1)} collective-permute-done((bf16[224,4096]{1,0:T(8,128)(2,1)}, bf16[224,4096]{1,0:T(8,128)(2,1)}, u32[]{:S(2)}, u32[]{:S(2)}) %collective-permute-start.23) | collective-permute-done | bytes 1835040 | tf_op jit(solution)/shard_map/ppermute | solution.py:288
  183.5 1.3 collective-permute-start.24
  184.8 2.0 collective-permute-start.26
  186.7 3.2 multiply_reduce_fusion
  190.0 6.0 %collective-permute-done.7.refs_2_ = bf16[5,224,128]{2,1,0:T(8,128)(2,1)S(1)} collective-permute-done((bf16[5,224,128]{2,1,0:T(8,128)(2,1)S(1)}, bf16[5,224,128]{2,1,0:T(8,128)(2,1)S(1)}, u32[]{:S(2)}, u32[]{:S(2)}) %collective-permute-start.7) | collective-permute-done | bytes 286752 | tf_op jit(solution)/shard_map/ppermute | solution.py:288
  196.1 4.2 %collective-permute-done.6.refs_1_ = bf16[5,224,128]{2,1,0:T(8,128)(2,1)S(1)} collective-permute-done((bf16[5,224,128]{2,1,0:T(8,128)(2,1)S(1)}, bf16[5,224,128]{2,1,0:T(8,128)(2,1)S(1)}, u32[]{:S(2)}, u32[]{:S(2)}) %collective-permute-start.6) | collective-permute-done | bytes 286752 | tf_op jit(solution)/shard_map/ppermute | solution.py:288
  200.2 5.4 %late.2 = (f32[2,224,4096]{2,1,0:T(8,128)}, bf16[4,2,224,4096]{3,2,1,0:T(8,128)(2,1)}, bf16[224,2048]{1,0:T(8,128)(2,1)S(1)}) custom-call(s32[17]{0:T(128)S(1)} %pad_add_fusion.scalars, bf16[4,2,224,128]{3,2,1,0:T(8,128)(2,1)S(1)} %bitcast.53, bf16[5,224,128]{2,1,0:T(8,128)(2,1)S(1)} %collective-permute-done.6.refs_1_, ...), custom_call_target="tpu_custom_call" | custom-call | flops 469762048 | bytes 6422528 | tf_op jit(solution)/shard_map/late/pallas_call | solution.py:175
  205.6 4.5 %collective-permute-start.28 = (bf16[224,2048]{1,0:T(8,128)(2,1)S(1)}, bf16[224,2048]{1,0:T(8,128)(2,1)S(1)}, u32[]{:S(2)}, u32[]{:S(2)}) collective-permute-start(bf16[224,2048]{1,0:T(8,128)(2,1)S(1)} %get-tuple-element.31), channel_id=1, source_target_pairs={{0,8},{8,16},{16,24},{1,9},{9,17},{17,25},{2,10},{10,18},{18,26},{... | collective-permute-start | bytes 2752520 | tf_op jit(solution)/shard_map/ppermute | solution.py:304
  210.1 1.3 collective-permute-start.27
  211.5 5.4 %late.3 = (f32[2,224,4096]{2,1,0:T(8,128)}, bf16[4,2,224,4096]{3,2,1,0:T(8,128)(2,1)}, bf16[224,2048]{1,0:T(8,128)(2,1)S(1)}) custom-call(s32[17]{0:T(128)S(1)} %pad_add_fusion.scalars, bf16[4,2,224,128]{3,2,1,0:T(8,128)(2,1)S(1)} %bitcast.54, ...), custom_call_target="tpu_custom_call", output_to_operand_aliasing={{0}: (10, {}), {1}: (11, {})} | custom-call | flops 469762048 | bytes 6422528 | tf_op jit(solution)/shard_map/late/pallas_call | solution.py:175
  216.9 4.6 %collective-permute-start.22 = (bf16[224,2048]{1,0:T(8,128)(2,1)S(1)}, bf16[224,2048]{1,0:T(8,128)(2,1)S(1)}, u32[]{:S(2)}, u32[]{:S(2)}) collective-permute-start(bf16[224,2048]{1,0:T(8,128)(2,1)S(1)} %get-tuple-element.26), channel_id=1, source_target_pairs={{0,8},{8,16},{16,24},{1,9},{9,17},{17,25},{2,10},{10,18},{18,26},{... | collective-permute-start | bytes 2752520 | tf_op jit(solution)/shard_map/ppermute | solution.py:304
  221.5 9.3 %collective-permute-done.28 = bf16[224,2048]{1,0:T(8,128)(2,1)S(1)} collective-permute-done((bf16[224,2048]{1,0:T(8,128)(2,1)S(1)}, bf16[224,2048]{1,0:T(8,128)(2,1)S(1)}, u32[]{:S(2)}, u32[]{:S(2)}) %collective-permute-start.28) | collective-permute-done | bytes 917536 | tf_op jit(solution)/shard_map/ppermute | solution.py:304
  232.1 19.2 %residue.1 = bf16[1792,4096]{1,0:T(8,128)(2,1)} custom-call(s32[8]{0:T(128)S(1)} %or_or_fusion.1.slots, bf16[1792,4096]{1,0:T(8,128)(2,1)} %bitcast.63, bf16[1792,4096]{1,0:T(8,128)(2,1)} %bitcast.65, bf16[1792,128]{1,0:T(8,128)(2,1)S(1)} %convolution_convert_fusion.p_ref, bf16[8,256,512]{2,1,0:T(8,128)(2,1)S(1)} %get-tuple-element.32.refs_5_.r_ref), custom_call_target="tpu_custom_call" | custom-call | flops 1879048192 | bytes 44040192 | tf_op jit(solution)/shard_map/residue/pallas_call | solution.py:103
  253.3 17.2 %early.1 = (f32[2,224,4096]{2,1,0:T(8,128)}, bf16[4,2,224,4096]{3,2,1,0:T(8,128)(2,1)}) custom-call(s32[17]{0:T(128)} %copy-done.6, bf16[4,2,224,128]{3,2,1,0:T(8,128)(2,1)} %bitcast.55, bf16[5,224,128]{2,1,0:T(8,128)(2,1)} %copy-done.4, bf16[5,224,128]{2,1,0:T(8,128)(2,1)} %copy-done.3, ...), custom_call_target="tpu_custom_call", output_to_operand_aliasing={{0}: (14, {}), {1}: (15, {})} | custom-call | flops 3758096384 | bytes 29360128 | tf_op jit(solution)/shard_map/early/pallas_call | solution.py:240
  270.5 4.6 %collective-permute-done.21 = bf16[224,2048]{1,0:T(8,128)(2,1)S(1)} collective-permute-done((bf16[224,2048]{1,0:T(8,128)(2,1)S(1)}, bf16[224,2048]{1,0:T(8,128)(2,1)S(1)}, u32[]{:S(2)}, u32[]{:S(2)}) %collective-permute-start.21) | collective-permute-done | bytes 917536 | tf_op jit(solution)/shard_map/ppermute | solution.py:303
  275.8 1.3 collective-permute-start.35
  277.1 1.3 collective-permute-start.31
  279.9 48.0 %collective-permute-done.35 = bf16[224,2048]{1,0:T(8,128)(2,1)S(1)} collective-permute-done((bf16[224,2048]{1,0:T(8,128)(2,1)S(1)}, bf16[224,2048]{1,0:T(8,128)(2,1)S(1)}, u32[]{:S(2)}, u32[]{:S(2)}) %collective-permute-start.35) | collective-permute-done | bytes 917536 | tf_op jit(solution)/shard_map/ppermute | solution.py:303
  328.0 1.3 collective-permute-start.36
  329.2 18.4 %collective-permute-done.31 = bf16[224,2048]{1,0:T(8,128)(2,1)S(1)} collective-permute-done((bf16[224,2048]{1,0:T(8,128)(2,1)S(1)}, bf16[224,2048]{1,0:T(8,128)(2,1)S(1)}, u32[]{:S(2)}, u32[]{:S(2)}) %collective-permute-start.31) | collective-permute-done | bytes 917536 | tf_op jit(solution)/shard_map/ppermute | solution.py:303
  351.5 29.9 %collective-permute-done.32 = bf16[224,2048]{1,0:T(8,128)(2,1)S(1)} collective-permute-done((bf16[224,2048]{1,0:T(8,128)(2,1)S(1)}, bf16[224,2048]{1,0:T(8,128)(2,1)S(1)}, u32[]{:S(2)}, u32[]{:S(2)}) %collective-permute-start.32) | collective-permute-done | bytes 917536 | tf_op jit(solution)/shard_map/ppermute | solution.py:303
  (95 shorter events, 27.7 us)
Async XLA Ops:
  1.6 6.6 %collective-permute-start = (bf16[1,512,128]{2,1,0:T(8,128)(2,1)S(1)}, bf16[1,512,128]{2,1,0:T(8,128)(2,1)S(1)}, u32[]{:S(2)}, u32[]{:S(2)}) collective-permute-start(bf16[1,512,128]{2,1,0:T(8,128)(2,1)S(1)} %convert_element_type.24), channel_id=1, source_target_pairs={{0,4},{1,5},{2,6},{3,7},{4,0},{5,1},{6,2},{7,3},{8,12},{9,13},{10,... | collective-permute-start | bytes 393224 | tf_op jit(solution)/shard_map/ppermute | solution.py:269
  8.2 7.5 %collective-permute-start.1 = (bf16[2,512,128]{2,1,0:T(8,128)(2,1)S(1)}, bf16[2,512,128]{2,1,0:T(8,128)(2,1)S(1)}, u32[]{:S(2)}, u32[]{:S(2)}) collective-permute-start(bf16[2,512,128]{2,1,0:T(8,128)(2,1)S(1)} %pad_maximum_fusion.11), channel_id=1, source_target_pairs={{0,2},{1,3},{2,0},{3,1},{4,6},{5,7},{6,4},{7,5},{8,10},{9,11},{10,... | collective-permute-start | bytes 786440 | tf_op jit(solution)/shard_map/ppermute | solution.py:269
  15.8 2.0 collective-permute-start.2
  33.9 4.5 %collective-permute-start.9 = (f32[4,128,512]{2,1,0:T(8,128)}, f32[4,128,512]{2,1,0:T(8,128)}, u32[]{:S(2)}, u32[]{:S(2)}) collective-permute-start(f32[4,128,512]{2,1,0:T(8,128)} %slice.46), channel_id=1, source_target_pairs={{0,1},{1,0},{2,3},{3,2},{4,5},{5,4},{6,7},{7,6},{8,9},{9,8},{10,11... | collective-permute-start | bytes 3145736 | tf_op jit(solution)/shard_map/ppermute | solution.py:269
  34.1 2.8 collective-permute-start.3
  36.9 4.6 %collective-permute-start.4 = (f32[128,128]{0,1:T(8,128)S(1)}, f32[128,128]{0,1:T(8,128)S(1)}, u32[]{:S(2)}, u32[]{:S(2)}) collective-permute-start(f32[128,128]{0,1:T(8,128)S(1)} %add.110), channel_id=1, source_target_pairs={{0,2},{1,3},{2,0},{3,1},{4,6},{5,7},{6,4},{7,5},{8,10},{9,11},{10,... | collective-permute-start | bytes 196616 | tf_op jit(solution)/shard_map/ppermute | solution.py:269
  39.8 1.0 copy-start.7
  40.8 17.5 %collective-permute-start.10 = (f32[2,128,512]{2,1,0:T(8,128)S(1)}, f32[2,128,512]{2,1,0:T(8,128)S(1)}, u32[]{:S(2)}, u32[]{:S(2)}) collective-permute-start(f32[2,128,512]{2,1,0:T(8,128)S(1)} %slice.55), channel_id=1, source_target_pairs={{0,2},{1,3},{2,0},{3,1},{4,6},{5,7},{6,4},{7,5},{8,10},{9,11},{10,... | collective-permute-start | bytes 1572872 | tf_op jit(solution)/shard_map/ppermute | solution.py:269
  41.5 4.3 %collective-permute-start.5 = (f32[128,128]{0,1:T(8,128)S(1)}, f32[128,128]{0,1:T(8,128)S(1)}, u32[]{:S(2)}, u32[]{:S(2)}) collective-permute-start(f32[128,128]{0,1:T(8,128)S(1)} %add.111), channel_id=1, source_target_pairs={{0,4},{1,5},{2,6},{3,7},{4,0},{5,1},{6,2},{7,3},{8,12},{9,13},{10,... | collective-permute-start | bytes 196616 | tf_op jit(solution)/shard_map/ppermute | solution.py:269
  59.5 12.2 %collective-permute-start.11 = (f32[1,128,512]{2,1,0:T(8,128)S(1)}, f32[1,128,512]{2,1,0:T(8,128)S(1)}, u32[]{:S(2)}, u32[]{:S(2)}) collective-permute-start(f32[1,128,512]{2,1,0:T(8,128)S(1)} %slice.57), channel_id=1, source_target_pairs={{0,4},{1,5},{2,6},{3,7},{4,0},{5,1},{6,2},{7,3},{8,12},{9,13},{10,... | collective-permute-start | bytes 786440 | tf_op jit(solution)/shard_map/ppermute | solution.py:269
  72.1 7.6 %collective-permute-start.12 = (bf16[1,128,512]{2,1,0:T(8,128)(2,1)S(1)}, bf16[1,128,512]{2,1,0:T(8,128)(2,1)S(1)}, u32[]{:S(2)}, u32[]{:S(2)}) collective-permute-start(bf16[1,128,512]{2,1,0:T(8,128)(2,1)S(1)} %fusion), channel_id=1, source_target_pairs={{0,24},{8,0},{16,8},{24,16},{1,25},{9,1},{17,9},{25,17},{2,26},{10... | collective-permute-start | bytes 393224 | tf_op jit(solution)/shard_map/ppermute | solution.py:288
  75.8 9.0 %collective-permute-start.16 = (bf16[1,128,512]{2,1,0:T(8,128)(2,1)S(1)}, bf16[1,128,512]{2,1,0:T(8,128)(2,1)S(1)}, u32[]{:S(2)}, u32[]{:S(2)}) collective-permute-start(bf16[1,128,512]{2,1,0:T(8,128)(2,1)S(1)} %fusion), channel_id=1, source_target_pairs={{0,16},{8,24},{16,0},{24,8},{1,17},{9,25},{17,1},{25,9},{2,18},{10... | collective-permute-start | bytes 393224 | tf_op jit(solution)/shard_map/ppermute | solution.py:288
  79.7 9.3 %collective-permute-start.13 = (bf16[1,256,512]{2,1,0:T(8,128)(2,1)S(1)}, bf16[1,256,512]{2,1,0:T(8,128)(2,1)S(1)}, u32[]{:S(2)}, u32[]{:S(2)}) collective-permute-start(bf16[1,256,512]{2,1,0:T(8,128)(2,1)S(1)} %pad_maximum_fusion.12), channel_id=1, source_target_pairs={{0,4},{1,5},{2,6},{3,7},{4,0},{5,1},{6,2},{7,3},{8,12},{9,13},{10,... | collective-permute-start | bytes 786440 | tf_op jit(solution)/shard_map/ppermute | solution.py:269
  79.9 7.2 %collective-permute-start.17 = (bf16[1,128,512]{2,1,0:T(8,128)(2,1)S(1)}, bf16[1,128,512]{2,1,0:T(8,128)(2,1)S(1)}, u32[]{:S(2)}, u32[]{:S(2)}) collective-permute-start(bf16[1,128,512]{2,1,0:T(8,128)(2,1)S(1)} %fusion), channel_id=1, source_target_pairs={{0,8},{8,16},{16,24},{24,0},{1,9},{9,17},{17,25},{25,1},{2,10},{10... | collective-permute-start | bytes 393224 | tf_op jit(solution)/shard_map/ppermute | solution.py:288
  87.1 9.2 %collective-permute-start.18 = (bf16[1,256,512]{2,1,0:T(8,128)(2,1)S(1)}, bf16[1,256,512]{2,1,0:T(8,128)(2,1)S(1)}, u32[]{:S(2)}, u32[]{:S(2)}) collective-permute-start(bf16[1,256,512]{2,1,0:T(8,128)(2,1)S(1)} %constant_dynamic-update-slice_fusion), channel_id=1, source_target_pairs={{0,2},{1,3},{2,0},{3,1},{4,6},{5,7},{6,4},{7,5},{8,10},{9,11},{10,... | collective-permute-start | bytes 786440 | tf_op jit(solution)/shard_map/ppermute | solution.py:269
  89.0 14.1 %collective-permute-start.14 = (bf16[2,256,512]{2,1,0:T(8,128)(2,1)S(1)}, bf16[2,256,512]{2,1,0:T(8,128)(2,1)S(1)}, u32[]{:S(2)}, u32[]{:S(2)}) collective-permute-start(bf16[2,256,512]{2,1,0:T(8,128)(2,1)S(1)} %pad_maximum_fusion.6), channel_id=1, source_target_pairs={{0,2},{1,3},{2,0},{3,1},{4,6},{5,7},{6,4},{7,5},{8,10},{9,11},{10,... | collective-permute-start | bytes 1572872 | tf_op jit(solution)/shard_map/ppermute | solution.py:269
  92.8 90.6 %collective-permute-start.23 = (bf16[224,4096]{1,0:T(8,128)(2,1)}, bf16[224,4096]{1,0:T(8,128)(2,1)}, u32[]{:S(2)}, u32[]{:S(2)}) collective-permute-start(bf16[224,4096]{1,0:T(8,128)(2,1)} %slice.67), channel_id=1, source_target_pairs={{0,24},{8,0},{16,8},{24,16},{1,25},{9,1},{17,9},{25,17},{2,26},{10... | collective-permute-start | bytes 5505032 | tf_op jit(solution)/shard_map/ppermute | solution.py:288
  95.6 87.8 %collective-permute-start.25 = (bf16[224,4096]{1,0:T(8,128)(2,1)}, bf16[224,4096]{1,0:T(8,128)(2,1)}, u32[]{:S(2)}, u32[]{:S(2)}) collective-permute-start(bf16[224,4096]{1,0:T(8,128)(2,1)} %slice.67), channel_id=1, source_target_pairs={{0,8},{8,16},{16,24},{24,0},{1,9},{9,17},{17,25},{25,1},{2,10},{10... | collective-permute-start | bytes 5505032 | tf_op jit(solution)/shard_map/ppermute | solution.py:288
  97.2 9.4 %collective-permute-start.19 = (bf16[2,256,512]{2,1,0:T(8,128)(2,1)}, bf16[2,256,512]{2,1,0:T(8,128)(2,1)S(1)}, u32[]{:S(2)}, u32[]{:S(2)}) collective-permute-start(bf16[2,256,512]{2,1,0:T(8,128)(2,1)} %pad_maximum_fusion.7), channel_id=1, source_target_pairs={{0,4},{1,5},{2,6},{3,7},{4,0},{5,1},{6,2},{7,3},{8,12},{9,13},{10,... | collective-permute-start | bytes 1572872 | tf_op jit(solution)/shard_map/ppermute | solution.py:269
  104.2 7.0 %collective-permute-start.15 = (bf16[4,256,512]{2,1,0:T(8,128)(2,1)}, bf16[4,256,512]{2,1,0:T(8,128)(2,1)}, u32[]{:S(2)}, u32[]{:S(2)}) collective-permute-start(bf16[4,256,512]{2,1,0:T(8,128)(2,1)} %pad_maximum_fusion.3), channel_id=1, source_target_pairs={{0,1},{1,0},{2,3},{3,2},{4,5},{5,4},{6,7},{7,6},{8,9},{9,8},{10,11... | collective-permute-start | bytes 3145736 | tf_op jit(solution)/shard_map/ppermute | solution.py:269
  107.7 77.1 %collective-permute-start.20 = (bf16[4,256,512]{2,1,0:T(8,128)(2,1)}, bf16[4,256,512]{2,1,0:T(8,128)(2,1)}, u32[]{:S(2)}, u32[]{:S(2)}) collective-permute-start(bf16[4,256,512]{2,1,0:T(8,128)(2,1)} %pad_maximum_fusion.4), channel_id=1, source_target_pairs={{0,1},{1,0},{2,3},{3,2},{4,5},{5,4},{6,7},{7,6},{8,9},{9,8},{10,11... | collective-permute-start | bytes 3145736 | tf_op jit(solution)/shard_map/ppermute | solution.py:269
  107.8 103.7 %copy-start.6 = (s32[17]{0:T(128)}, s32[17]{0:T(128)S(1)}, u32[]{:S(2)}) copy-start(s32[17]{0:T(128)S(1)} %pad_add_fusion.scalars) | copy-start | bytes 208
  108.6 123.4 %copy-start.1 = (bf16[1792,128]{1,0:T(8,128)(2,1)}, bf16[1792,128]{1,0:T(8,128)(2,1)S(1)}, u32[]{:S(2)}) copy-start(bf16[1792,128]{1,0:T(8,128)(2,1)S(1)} %convolution_convert_fusion.p_ref) | copy-start | bytes 1376260
  108.8 81.2 %collective-permute-start.8 = (bf16[5,224,128]{2,1,0:T(8,128)(2,1)S(1)}, bf16[5,224,128]{2,1,0:T(8,128)(2,1)S(1)}, u32[]{:S(2)}, u32[]{:S(2)}) collective-permute-start(bf16[5,224,128]{2,1,0:T(8,128)(2,1)S(1)} %get-tuple-element.45), channel_id=1, source_target_pairs={{0,8},{8,16},{16,24},{24,0},{1,9},{9,17},{17,25},{25,1},{2,10},{10... | collective-permute-start | bytes 860168 | tf_op jit(solution)/shard_map/ppermute | solution.py:288
  111.2 84.9 %collective-permute-start.7 = (bf16[5,224,128]{2,1,0:T(8,128)(2,1)S(1)}, bf16[5,224,128]{2,1,0:T(8,128)(2,1)S(1)}, u32[]{:S(2)}, u32[]{:S(2)}) collective-permute-start(bf16[5,224,128]{2,1,0:T(8,128)(2,1)S(1)} %get-tuple-element.46), channel_id=1, source_target_pairs={{0,16},{8,24},{16,0},{24,8},{1,17},{9,25},{17,1},{25,9},{2,18},{10... | collective-permute-start | bytes 860168 | tf_op jit(solution)/shard_map/ppermute | solution.py:288
  114.4 117.7 %copy-start = (bf16[8,256,512]{2,1,0:T(8,128)(2,1)}, bf16[8,256,512]{2,1,0:T(8,128)(2,1)S(1)}, u32[]{:S(2)}) copy-start(bf16[8,256,512]{2,1,0:T(8,128)(2,1)S(1)} %get-tuple-element.32.refs_5_.r_ref) | copy-start | bytes 6291460
  183.5 16.7 %collective-permute-start.6 = (bf16[5,224,128]{2,1,0:T(8,128)(2,1)S(1)}, bf16[5,224,128]{2,1,0:T(8,128)(2,1)S(1)}, u32[]{:S(2)}, u32[]{:S(2)}) collective-permute-start(bf16[5,224,128]{2,1,0:T(8,128)(2,1)S(1)} %get-tuple-element.47), channel_id=1, source_target_pairs={{0,24},{8,0},{16,8},{24,16},{1,25},{9,1},{17,9},{25,17},{2,26},{10... | collective-permute-start | bytes 860168 | tf_op jit(solution)/shard_map/ppermute | solution.py:288
  183.5 68.5 %collective-permute-start.24 = (bf16[224,4096]{1,0:T(8,128)(2,1)}, bf16[224,4096]{1,0:T(8,128)(2,1)S(1)}, u32[]{:S(2)}, u32[]{:S(2)}) collective-permute-start(bf16[224,4096]{1,0:T(8,128)(2,1)} %collective-permute-done.23.refs_9_), channel_id=1, source_target_pairs={{8,0},{16,8},{9,1},{17,9},{10,2},{18,10},{11,3},{19,11},{12,4},{20... | collective-permute-start | bytes 5505032 | tf_op jit(solution)/shard_map/ppermute | solution.py:296
  184.8 67.2 %collective-permute-start.26 = (bf16[224,4096]{1,0:T(8,128)(2,1)}, bf16[224,4096]{1,0:T(8,128)(2,1)}, u32[]{:S(2)}, u32[]{:S(2)}) collective-permute-start(bf16[224,4096]{1,0:T(8,128)(2,1)} %collective-permute-done.25.refs_12_), channel_id=1, source_target_pairs={{8,16},{16,24},{9,17},{17,25},{10,18},{18,26},{11,19},{19,27},{12,... | collective-permute-start | bytes 5505032 | tf_op jit(solution)/shard_map/ppermute | solution.py:297
  190.0 21.4 %copy-start.5 = (f32[1,512]{1,0:T(1,128)}, f32[1,512]{1,0:T(1,128)S(1)}, u32[]{:S(2)}) copy-start(f32[1,512]{1,0:T(1,128)S(1)} %fusion.8.refs_4_) | copy-start | bytes 6148
  190.0 21.4 %copy-start.2 = (bf16[5,224,128]{2,1,0:T(8,128)(2,1)}, bf16[5,224,128]{2,1,0:T(8,128)(2,1)S(1)}, u32[]{:S(2)}) copy-start(bf16[5,224,128]{2,1,0:T(8,128)(2,1)S(1)} %collective-permute-done.8.refs_3_) | copy-start | bytes 860164
  196.1 15.4 %copy-start.3 = (bf16[5,224,128]{2,1,0:T(8,128)(2,1)}, bf16[5,224,128]{2,1,0:T(8,128)(2,1)S(1)}, u32[]{:S(2)}) copy-start(bf16[5,224,128]{2,1,0:T(8,128)(2,1)S(1)} %collective-permute-done.7.refs_2_) | copy-start | bytes 860164
  200.2 11.2 %copy-start.4 = (bf16[5,224,128]{2,1,0:T(8,128)(2,1)}, bf16[5,224,128]{2,1,0:T(8,128)(2,1)S(1)}, u32[]{:S(2)}) copy-start(bf16[5,224,128]{2,1,0:T(8,128)(2,1)S(1)} %collective-permute-done.6.refs_1_) | copy-start | bytes 860164
  205.6 25.2 %collective-permute-start.28 = (bf16[224,2048]{1,0:T(8,128)(2,1)S(1)}, bf16[224,2048]{1,0:T(8,128)(2,1)S(1)}, u32[]{:S(2)}, u32[]{:S(2)}) collective-permute-start(bf16[224,2048]{1,0:T(8,128)(2,1)S(1)} %get-tuple-element.31), channel_id=1, source_target_pairs={{0,8},{8,16},{16,24},{1,9},{9,17},{17,25},{2,10},{10,18},{18,26},{... | collective-permute-start | bytes 2752520 | tf_op jit(solution)/shard_map/ppermute | solution.py:304
  210.1 41.2 %collective-permute-start.27 = (bf16[224,2048]{1,0:T(8,128)(2,1)S(1)}, bf16[224,2048]{1,0:T(8,128)(2,1)S(1)}, u32[]{:S(2)}, u32[]{:S(2)}) collective-permute-start(bf16[224,2048]{1,0:T(8,128)(2,1)S(1)} %get-tuple-element.31), channel_id=1, source_target_pairs={{8,0},{16,8},{24,16},{9,1},{17,9},{25,17},{10,2},{18,10},{26,18},{... | collective-permute-start | bytes 2752520 | tf_op jit(solution)/shard_map/ppermute | solution.py:303
  216.9 53.6 %collective-permute-start.22 = (bf16[224,2048]{1,0:T(8,128)(2,1)S(1)}, bf16[224,2048]{1,0:T(8,128)(2,1)S(1)}, u32[]{:S(2)}, u32[]{:S(2)}) collective-permute-start(bf16[224,2048]{1,0:T(8,128)(2,1)S(1)} %get-tuple-element.26), channel_id=1, source_target_pairs={{0,8},{8,16},{16,24},{1,9},{9,17},{17,25},{2,10},{10,18},{18,26},{... | collective-permute-start | bytes 2752520 | tf_op jit(solution)/shard_map/ppermute | solution.py:304
  230.8 44.3 %collective-permute-start.21 = (bf16[224,2048]{1,0:T(8,128)(2,1)S(1)}, bf16[224,2048]{1,0:T(8,128)(2,1)S(1)}, u32[]{:S(2)}, u32[]{:S(2)}) collective-permute-start(bf16[224,2048]{1,0:T(8,128)(2,1)S(1)} %get-tuple-element.26), channel_id=1, source_target_pairs={{8,0},{16,8},{24,16},{9,1},{17,9},{25,17},{10,2},{18,10},{26,18},{... | collective-permute-start | bytes 2752520 | tf_op jit(solution)/shard_map/ppermute | solution.py:303
  251.3 27.1 %collective-permute-start.29 = (bf16[224,2048]{1,0:T(8,128)(2,1)S(1)}, bf16[224,2048]{1,0:T(8,128)(2,1)S(1)}, u32[]{:S(2)}, u32[]{:S(2)}) collective-permute-start(bf16[224,2048]{1,0:T(8,128)(2,1)S(1)} %collective-permute-done.28), channel_id=1, source_target_pairs={{8,16},{16,24},{9,17},{17,25},{10,18},{18,26},{11,19},{19,27},{12,... | collective-permute-start | bytes 2752520 | tf_op jit(solution)/shard_map/ppermute | solution.py:304
  252.0 1.2 copy-start.8
  275.1 4.1 %collective-permute-start.33 = (bf16[224,2048]{1,0:T(8,128)(2,1)S(1)}, bf16[224,2048]{1,0:T(8,128)(2,1)S(1)}, u32[]{:S(2)}, u32[]{:S(2)}) collective-permute-start(bf16[224,2048]{1,0:T(8,128)(2,1)S(1)} %collective-permute-done.22), channel_id=1, source_target_pairs={{8,16},{16,24},{9,17},{17,25},{10,18},{18,26},{11,19},{19,27},{12,... | collective-permute-start | bytes 2752520 | tf_op jit(solution)/shard_map/ppermute | solution.py:304
  275.8 52.1 %collective-permute-start.35 = (bf16[224,2048]{1,0:T(8,128)(2,1)S(1)}, bf16[224,2048]{1,0:T(8,128)(2,1)S(1)}, u32[]{:S(2)}, u32[]{:S(2)}) collective-permute-start(bf16[224,2048]{1,0:T(8,128)(2,1)S(1)} %collective-permute-done.21), channel_id=1, source_target_pairs={{8,0},{16,8},{9,1},{17,9},{10,2},{18,10},{11,3},{19,11},{12,4},{20... | collective-permute-start | bytes 2752520 | tf_op jit(solution)/shard_map/ppermute | solution.py:303
  277.1 70.5 %collective-permute-start.31 = (bf16[224,2048]{1,0:T(8,128)(2,1)S(1)}, bf16[224,2048]{1,0:T(8,128)(2,1)S(1)}, u32[]{:S(2)}, u32[]{:S(2)}) collective-permute-start(bf16[224,2048]{1,0:T(8,128)(2,1)S(1)} %collective-permute-done.27), channel_id=1, source_target_pairs={{8,0},{16,8},{9,1},{17,9},{10,2},{18,10},{11,3},{19,11},{12,4},{20... | collective-permute-start | bytes 2752520 | tf_op jit(solution)/shard_map/ppermute | solution.py:303
  278.4 70.5 %collective-permute-start.30 = (bf16[224,2048]{1,0:T(8,128)(2,1)S(1)}, bf16[224,2048]{1,0:T(8,128)(2,1)S(1)}, u32[]{:S(2)}, u32[]{:S(2)}) collective-permute-start(bf16[224,2048]{1,0:T(8,128)(2,1)S(1)} %collective-permute-done.29), channel_id=1, source_target_pairs={{16,24},{17,25},{18,26},{19,27},{20,28},{21,29},{22,30},{23,31}} | collective-permute-start | bytes 2752520 | tf_op jit(solution)/shard_map/ppermute | solution.py:304
  279.2 103.4 %collective-permute-start.34 = (bf16[224,2048]{1,0:T(8,128)(2,1)S(1)}, bf16[224,2048]{1,0:T(8,128)(2,1)S(1)}, u32[]{:S(2)}, u32[]{:S(2)}) collective-permute-start(bf16[224,2048]{1,0:T(8,128)(2,1)S(1)} %collective-permute-done.33), channel_id=1, source_target_pairs={{16,24},{17,25},{18,26},{19,27},{20,28},{21,29},{22,30},{23,31}} | collective-permute-start | bytes 2752520 | tf_op jit(solution)/shard_map/ppermute | solution.py:304
  328.0 57.2 %collective-permute-start.36 = (bf16[224,2048]{1,0:T(8,128)(2,1)S(1)}, bf16[224,2048]{1,0:T(8,128)(2,1)S(1)}, u32[]{:S(2)}, u32[]{:S(2)}) collective-permute-start(bf16[224,2048]{1,0:T(8,128)(2,1)S(1)} %collective-permute-done.35), channel_id=1, source_target_pairs={{8,0},{9,1},{10,2},{11,3},{12,4},{13,5},{14,6},{15,7}} | collective-permute-start | bytes 2752520 | tf_op jit(solution)/shard_map/ppermute | solution.py:303
  347.6 33.7 %collective-permute-start.32 = (bf16[224,2048]{1,0:T(8,128)(2,1)S(1)}, bf16[224,2048]{1,0:T(8,128)(2,1)S(1)}, u32[]{:S(2)}, u32[]{:S(2)}) collective-permute-start(bf16[224,2048]{1,0:T(8,128)(2,1)S(1)} %collective-permute-done.31), channel_id=1, source_target_pairs={{8,0},{9,1},{10,2},{11,3},{12,4},{13,5},{14,6},{15,7}} | collective-permute-start | bytes 2752520 | tf_op jit(solution)/shard_map/ppermute | solution.py:303

commit v2 on v1

--- a/solution.py
+++ b/solution.py
@@ -14,6 +14,8 @@
 outer_beta = 0.9
 outer_rate = 0.7
 epsilon = 1e-06
+EARLY = (3, 7)
+CUTS = 1
 bf16 = jnp.bfloat16
 f32 = jnp.float32
 
@@ -26,6 +28,10 @@
 
 def cost(flops, moved):
     return pl.CostEstimate(flops=int(flops), bytes_accessed=int(moved), transcendentals=0)
+
+
+def piece(shape, index):
+    return pl.BlockSpec(tuple(pl.Element(size) for size in shape), index)
 
 
 def divisor(total, most, step):
@@ -146,11 +152,11 @@
     def _():
         for d in range(n):
             at = slice(d * rank, (d + 1) * rank)
-            left[:, at] = scaled(p_refs[d][0, 0] if d == 0 else p_refs[d][0], scale[:, at])
-
-    momentum_new, anchor_new = outer(m_ref[0], a_ref[0, 0], change(left, low, high))
-    m_out[0] = momentum_new
-    a_out[0, 0] = anchor_new
+            left[:, at] = scaled(p_refs[d][0] if d == 0 else p_refs[d][...], scale[:, at])
+
+    momentum_new, anchor_new = outer(m_ref[...], a_ref[0], change(left, low, high))
+    m_out[...] = momentum_new
+    a_out[0] = anchor_new
     share[...] = anchor_new
 
 
@@ -164,21 +170,23 @@
     ]
 
 
-def late(scalars, own, others, scale, stacks, momentum, anchor, span, filled):
-    n, parts, height, _ = anchor.shape
+def late(scalars, own, others, scale, stacks, momentum, anchor, offset, span, filled):
+    n, quarter, _ = anchor.shape
+    height = quarter - offset
     width, depth, rank = stacks[0].shape[-1], scale.shape[-1], own.shape[-1]
-    last, (start, stop) = parts - 1, span
+    start, stop = span
     fixed = lambda *at: (lambda j, s: at)
-    m_spec = pl.BlockSpec((1, height, width), lambda j, s: (last, 0, start + j))
-    a_spec = pl.BlockSpec((1, 1, height, width), lambda j, s: (s[0], last, 0, start + j))
+    column = lambda j: (start + j) * width
+    m_spec = piece((height, width), lambda j, s: (offset, column(j)))
+    a_spec = piece((1, height, width), lambda j, s: (s[0], offset, column(j)))
     columns = (stop - start) * width
     return pl.pallas_call(
         functools.partial(late_kernel, n),
         grid_spec=pltpu.PrefetchScalarGridSpec(
             num_scalar_prefetch=1,
             grid=(stop - start,),
-            in_specs=[pl.BlockSpec((1, 1, height, rank), lambda j, s: (s[0], last, 0, 0))]
-            + [pl.BlockSpec((1, height, rank), fixed(last * n, 0, 0))] * (n - 1)
+            in_specs=[piece((1, height, rank), lambda j, s: (s[0], offset, 0))]
+            + [piece((height, rank), fixed(n * offset, 0))] * (n - 1)
             + [pl.BlockSpec((1, depth), fixed(0, 0)), *stack_specs(stacks, start), m_spec, a_spec]
             + [pl.BlockSpec(memory_space=pl.ANY)] * len(filled),
             out_specs=[m_spec, a_spec, pl.BlockSpec((height, width), lambda j, s: (0, j))],
@@ -208,43 +216,44 @@
         for d in range(n):
             at = slice(d * rank, (d + 1) * rank)
             for k in range(n):
-                rows = p_refs[d][k, 0] if d == 0 else p_refs[d][k]
-                left[k * height : (k + 1) * height, at] = scaled(rows, scale[:, at])
+                to = slice(k * height, (k + 1) * height)
+                left[to, at] = scaled(p_refs[d][k] if d == 0 else p_refs[d][to], scale[:, at])
 
     mean[...] = change(left, low, high).reshape(mean.shape)
     for d in range(n):
         k = lax.rem(scalars[0] + d, n)
         if d == 0:
-            momentum = m_ref[0]
+            momentum = m_ref[...]
         else:
             start = sum(counts[: d - 1])
             momentum = got[start][...].astype(f32)
             for ref in got[start + 1 : start + counts[d - 1]]:
                 momentum = momentum + ref[...].astype(f32)
-        momentum_new, anchor_new = outer(momentum, a_ref[k, 0], mean[k])
+        momentum_new, anchor_new = outer(momentum, a_ref[k], mean[k])
         if d == 0:
-            m_out[0] = momentum_new
-        a_out[k, 0] = anchor_new
-
-
-def early(scalars, own, others, scale, stacks, momentum, anchor, got, filled):
-    n, _, height, cols = anchor.shape
-    blocks, _, width = stacks[0].shape
+            m_out[...] = momentum_new
+        a_out[k] = anchor_new
+
+
+def early(scalars, own, others, scale, stacks, momentum, anchor, height, got, span, filled):
+    n, _, _ = anchor.shape
+    width, (start, stop) = stacks[0].shape[-1], span
     depth, rank = scale.shape[-1], own.shape[-1]
     counts = [len(pieces) for pieces in got]
     flat = [piece for pieces in got for piece in pieces]
     fixed = lambda *at: (lambda j, s: at)
-    m_spec = pl.BlockSpec((1, height, width), lambda j, s: (0, 0, j))
-    a_spec = pl.BlockSpec((n, 1, height, width), lambda j, s: (0, 0, 0, j))
+    column = lambda j: (start + j) * width
+    m_spec = piece((height, width), lambda j, s: (0, column(j)))
+    a_spec = piece((n, height, width), lambda j, s: (0, 0, column(j)))
     first_alias = n + 6 + len(flat)
     return pl.pallas_call(
         functools.partial(early_kernel, n, counts),
         grid_spec=pltpu.PrefetchScalarGridSpec(
             num_scalar_prefetch=1,
-            grid=(blocks,),
-            in_specs=[pl.BlockSpec((n, 1, height, rank), fixed(0, 0, 0, 0))]
-            + [pl.BlockSpec((n, height, rank), fixed(0, 0, 0))] * (n - 1)
-            + [pl.BlockSpec((1, depth), fixed(0, 0)), *stack_specs(stacks, 0), m_spec, a_spec]
+            grid=(stop - start,),
+            in_specs=[piece((n, height, rank), fixed(0, 0, 0))]
+            + [piece((n * height, rank), fixed(0, 0))] * (n - 1)
+            + [pl.BlockSpec((1, depth), fixed(0, 0)), *stack_specs(stacks, start), m_spec, a_spec]
             + [pl.BlockSpec((height, width), lambda j, s: (0, j))] * len(flat)
             + [pl.BlockSpec(memory_space=pl.ANY)] * 2,
             out_specs=[m_spec, a_spec],
@@ -259,7 +268,9 @@
         ],
         input_output_aliases={first_alias: 0, first_alias + 1: 1},
         compiler_params=params(56),
-        cost_estimate=cost(2 * n * height * cols * depth, 32 * height * cols),
+        cost_estimate=cost(
+            2 * n * height * (stop - start) * width * depth, 32 * height * (stop - start) * width
+        ),
         name="early",
     )(scalars, own, *others, scale, *stacks, momentum, anchor, *flat, *filled)
 
@@ -322,14 +333,15 @@
     rate = math.sqrt(rows * size * cols / rank)
 
     quarter = momentum.shape[0]
-    parts = 2 if quarter % 16 == 0 else 1
-    height = quarter // parts
-    momentum = momentum.reshape(parts, height, cols)
-    anchor = anchor.reshape(n, parts, height, cols)
     forward = n == 4
-    if parts == 2:
-        ahead = momentum[0].astype(bf16)
-        got = near(ahead) if forward else [from_island(ahead, d) for d in range(1, n)]
+    offset = quarter * EARLY[0] // EARLY[1] // 16 * 16 if forward else 0
+    anchor = anchor.reshape(n, quarter, cols)
+    count = 2 if forward and cols % 2048 == 0 else 1
+    got = []
+    cuts = CUTS if count == CUTS else 1
+    for k in range(cuts if offset else 0):
+        at = slice(k * cols // cuts, (k + 1) * cols // cuts)
+        got.append(near(momentum[:offset, at].astype(bf16)))
 
     bits = [1 << k for k in range(size.bit_length() - 1)]
     split = size == 1 << len(bits) and (cols // size) % 128 == 0
@@ -368,19 +380,17 @@
     pieces = [factor, *pieces]
 
     basis = exact(raw, upper_inverse).astype(bf16)
-    by_part = basis.reshape(n, parts, height, rank)
+    rows_of = basis.reshape(n, quarter, rank)
     others = []
     for d in range(1, n):
-        wanted = lax.dynamic_index_in_dim(by_part[:, -1], (island + n - d) % n, 0)
-        sent = jnp.concatenate([by_part[:, 0], wanted], 0) if parts == 2 else wanted
-        others.append(from_island(sent, d))
-
-    if parts == 2 and forward:
-        above, below = got
+        to = (island + n - d) % n
+        wanted = lax.dynamic_slice(rows_of, (to, offset, 0), (1, quarter - offset, rank))[0]
+        ahead = rows_of[:, :offset].reshape(n * offset, rank)
+        others.append(from_island(jnp.concatenate([ahead, wanted], 0), d))
+
+    for k, (above, below) in enumerate(got):
         down, up = onward(above, below)
-        got = [(above,), (down, up), (below,)]
-    elif parts == 2:
-        got = [(piece,) for piece in got]
+        got[k] = [(above,), (down, up), (below,)]
     stacks = [jnp.concatenate(pieces[:2], axis=1), jnp.concatenate(pieces[2:], axis=1)]
     if split:
         for pair in zip(falling, crossed):
@@ -389,11 +399,10 @@
     scale = ((rate / n) / jnp.sqrt(jnp.concatenate(squares) + epsilon))[None]
 
     first, filled = [], []
-    count = 2 if forward and blocks % 2 == 0 else 1
-    for k in range(count):
-        span = (k * blocks // count, (k + 1) * blocks // count)
+    spans = [(k * blocks // count, (k + 1) * blocks // count) for k in range(count)]
+    for span in spans:
         *filled, share = late(
-            scalars, by_part, others, scale, stacks, momentum, anchor, span, filled
+            scalars, rows_of, others, scale, stacks, momentum, anchor, offset, span, filled
         )
         if forward:
             first.append(line_step(share, share, 1))
@@ -403,9 +412,10 @@
     if forward:
         (*flat, buffer_new) = tie(*first[0], buffer_new)
         second = [line_step(*flat, 2)]
-    if parts == 2:
+    spans = [(k * blocks // cuts, (k + 1) * blocks // cuts) for k in range(cuts)]
+    for pieces, span in zip(got, spans):
         filled = early(
-            scalars, by_part, others, scale, stacks, momentum, anchor, got, filled
+            scalars, rows_of, others, scale, stacks, momentum, anchor, offset, pieces, span, filled
         )
     momentum_new, anchor_new = filled
     if forward:
@@ -423,13 +433,13 @@
         for d in found:
             anchor_new = lax.dynamic_update_slice(
                 anchor_new,
-                found[d][k][None, None],
-                ((island + d) % n, parts - 1, 0, k * cols // count),
+                found[d][k][None],
+                ((island + d) % n, offset, k * cols // count),
             )
     return (
         anchor_new.reshape(rows, cols),
         buffer_new[None],
-        momentum_new.reshape(quarter, cols),
+        momentum_new,
     )
 
 

time: 387 us -> 389 us (level)
    ppermute x1, waiting for transfers between devices: 0.01 us -> 11.1 us  [onward(): down = lax.ppermute(above, 'island', [(1, 0), (2, 1)])]
    ppermute x6, waiting for transfers between devices: 9.31 us -> 0.02 us  [line_step(): lax.ppermute(up, 'island', [(k, k + 1) for k in range(step - 1, n - 1)])]
    ppermute x6, waiting for transfers between devices: 101 us -> 93.4 us  [line_step(): lax.ppermute(down, 'island', [(k, k - 1) for k in range(1, n - step + 1)])]
    ppermute x15, waiting for transfers between devices: 23.5 us -> 29.8 us  [swap(): return lax.ppermute(x, 'fsdp', [(i, i ^ bit) for i in range(size)])]
  transfers between devices with their start and end apart: 37 -> 37, of which waited for: 19 -> 20; matrix products, arithmetic and copies ran while one was open for 11% -> 12% of each run, Pallas kernels for 12% -> 12%
where the time goes in v2:
time: 389 us; the launch traced here: 388 us
  waiting for transfers between devices  223 us (57%)
  Pallas kernels  61.1 us (16%)
  starting transfers between devices  49.5 us (13%)
  other arithmetic  44.5 us (11%)
  local copies, waits for them, and re-layouts  7.31 us (2%)
    ppermute x6, waiting for transfers between devices, line_step(): lax.ppermute(down, 'island', [(k, k - 1) for k in range(1, n - step + 1)])  93.4 us
    ppermute x8, waiting for transfers between devices, from_island(): return lax.ppermute(x, 'island', [(s, (s - ahead) % n) for s in range(n)])  88.6 us
    ppermute x15, waiting for transfers between devices, swap(): return lax.ppermute(x, 'fsdp', [(i, i ^ bit) for i in range(size)])  29.8 us
    pallas_call x1, Pallas kernels, residue(): pl.pallas_call(residue_kernel, grid_spec=pltpu.PrefetchScalarGridSpec(num...  19.2 us
    pallas_call x1, Pallas kernels, early(): pl.pallas_call(functools.partial(early_kernel, n, counts), grid_spec=pltp...  15.7 us
    pallas_call x1, Pallas kernels, project(): pl.pallas_call(project_kernel, grid_spec=pltpu.PrefetchScalarGridSpec(num...  14.9 us
    ppermute x8, starting transfers between devices, from_island(): return lax.ppermute(x, 'island', [(s, (s - ahead) % n) for s in range(n)])  14.9 us
    ppermute x15, starting transfers between devices, swap(): return lax.ppermute(x, 'fsdp', [(i, i ^ bit) for i in range(size)])  14.8 us
  transfers between devices with their start and end apart: 37, of which 20 were waited for; matrix products, arithmetic and copies ran while one was open for 12% of the time, Pallas kernels for 12%

profile of v2, /device:TPU:0, one launch (start us, length us, event | category | flops | bytes accessed | tf_op | source)
XLA Modules:
  0.0 388.0 jit_solution(12724949608222470196)
XLA Ops:
  1.6 3.1 collective-permute-start
  4.7 3.5 collective-permute-done
  8.2 1.8 collective-permute-start.1
  10.0 5.8 %collective-permute-done.1 = bf16[2,512,128]{2,1,0:T(8,128)(2,1)S(1)} collective-permute-done((bf16[2,512,128]{2,1,0:T(8,128)(2,1)S(1)}, bf16[2,512,128]{2,1,0:T(8,128)(2,1)S(1)}, u32[]{:S(2)}, u32[]{:S(2)}) %collective-permute-start.1) | collective-permute-done | bytes 262176 | tf_op jit(solution)/shard_map/ppermute | solution.py:280
  15.9 1.9 collective-permute-done.2
  17.9 14.9 %project.1 = (f32[1792,128]{1,0:T(8,128)S(1)}, f32[8,128,512]{2,1,0:T(8,128)S(1)}, f32[128,128]{1,0:T(8,128)S(1)}) custom-call(s32[8]{0:T(128)S(1)} %or_or_fusion.1.slots, bf16[1792,4096]{1,0:T(8,128)(2,1)} %bitcast.55, bf16[1792,4096]{1,0:T(8,128)(2,1)} %bitcast.57, bf16[8,512,128]{2,1,0:T(8,128)(2,1)S(1)} %pad_maximum_fusion.2.q_ref), custom_call_target="tpu_custom_call" | custom-call | flops 3758096384 | bytes 29360128 | tf_op jit(solution)/shard_map/project/pallas_call | solution.py:69
  34.5 2.3 collective-permute-done.3
  36.9 1.5 collective-permute-start.4
  38.4 1.5 slice_add_fusion
  41.5 1.5 collective-permute-start.5
  43.0 2.8 collective-permute-done.5
  46.0 11.7 %cholesky.17 = f32[128,128]{1,0:T(8,128)S(1)} custom-call(f32[128,128]{1,0:T(8,128)S(1)} %fusion.6), custom_call_target="Cholesky" | custom-call | tf_op jit(solution)/shard_map/jit(cholesky)/cholesky | solution.py:372
  59.6 1.5 collective-permute-start.11
  61.7 9.8 %custom-call.6 = f32[1,128,128]{1,2,0:T(8,128)S(1)} custom-call(f32[1,128,128]{2,1,0:T(8,128)S(1)} %fusion.3), custom_call_target="InvertDiagBlocksLowerTriangular" | custom-call | tf_op jit(solution)/shard_map/triangular_solve | solution.py:373
  72.2 3.7 collective-permute-start.12
  75.8 3.9 %collective-permute-done.12 = bf16[1,128,512]{2,1,0:T(8,128)(2,1)S(1)} collective-permute-done((bf16[1,128,512]{2,1,0:T(8,128)(2,1)S(1)}, bf16[1,128,512]{2,1,0:T(8,128)(2,1)S(1)}, u32[]{:S(2)}, u32[]{:S(2)}) %collective-permute-start.12) | collective-permute-done | bytes 131104 | tf_op jit(solution)/shard_map/ppermute | solution.py:299
  79.9 4.6 %collective-permute-start.17 = (bf16[1,128,512]{2,1,0:T(8,128)(2,1)S(1)}, bf16[1,128,512]{2,1,0:T(8,128)(2,1)S(1)}, u32[]{:S(2)}, u32[]{:S(2)}) collective-permute-start(bf16[1,128,512]{2,1,0:T(8,128)(2,1)S(1)} %fusion), channel_id=1, source_target_pairs={{0,8},{8,16},{16,24},{24,0},{1,9},{9,17},{17,25},{25,1},{2,10},{10... | collective-permute-start | bytes 393224 | tf_op jit(solution)/shard_map/ppermute | solution.py:299
  84.8 2.3 collective-permute-done.17
  87.1 1.9 collective-permute-start.18
  89.3 7.0 %collective-permute-done.18 = bf16[1,256,512]{2,1,0:T(8,128)(2,1)S(1)} collective-permute-done((bf16[1,256,512]{2,1,0:T(8,128)(2,1)S(1)}, bf16[1,256,512]{2,1,0:T(8,128)(2,1)S(1)}, u32[]{:S(2)}, u32[]{:S(2)}) %collective-permute-start.18) | collective-permute-done | bytes 262176 | tf_op jit(solution)/shard_map/ppermute | solution.py:280
  96.4 1.8 collective-permute-start.19
  98.2 5.0 %collective-permute-done.14 = bf16[2,256,512]{2,1,0:T(8,128)(2,1)S(1)} collective-permute-done((bf16[2,256,512]{2,1,0:T(8,128)(2,1)S(1)}, bf16[2,256,512]{2,1,0:T(8,128)(2,1)S(1)}, u32[]{:S(2)}, u32[]{:S(2)}) %collective-permute-start.14) | collective-permute-done | bytes 524320 | tf_op jit(solution)/shard_map/ppermute | solution.py:280
  104.2 1.4 collective-permute-done.19
  106.8 3.2 slice.58
  110.0 2.0 collective-permute-start.23
  113.4 3.6 collective-permute-start.6
  117.0 1.9 multiply_reduce_fusion.1
  119.6 3.2 multiply_reduce_fusion
  122.8 64.1 %collective-permute-done.6.refs_1_ = bf16[1024,128]{1,0:T(8,128)(2,1)S(1)} collective-permute-done((bf16[1024,128]{1,0:T(8,128)(2,1)S(1)}, bf16[1024,128]{1,0:T(8,128)(2,1)S(1)}, u32[]{:S(2)}, u32[]{:S(2)}) %collective-permute-start.6) | collective-permute-done | bytes 262176 | tf_op jit(solution)/shard_map/ppermute | solution.py:299
  186.9 18.0 %collective-permute-done.7.refs_2_ = bf16[1024,128]{1,0:T(8,128)(2,1)S(1)} collective-permute-done((bf16[1024,128]{1,0:T(8,128)(2,1)S(1)}, bf16[1024,128]{1,0:T(8,128)(2,1)S(1)}, u32[]{:S(2)}, u32[]{:S(2)}) %collective-permute-start.7) | collective-permute-done | bytes 262176 | tf_op jit(solution)/shard_map/ppermute | solution.py:299
  205.0 5.7 %late.2 = (f32[448,4096]{1,0:T(8,128)}, bf16[4,448,4096]{2,1,0:T(8,128)(2,1)}, bf16[256,2048]{1,0:T(8,128)(2,1)S(1)}) custom-call(s32[17]{0:T(128)S(1)} %pad_add_fusion.scalars, bf16[4,448,128]{2,1,0:T(8,128)(2,1)S(1)} %bitcast.49, bf16[1024,128]{1,0:T(8,128)(2,1)S(1)} %collective-permute-done.6.refs_1_, ...), custom_call_target="tpu_custom_call" | custom-call | flops 536870912 | bytes 7340032 | tf_op jit(solution)/shard_map/late/pallas_call | solution.py:183
  211.9 4.6 %collective-permute-start.28 = (bf16[256,2048]{1,0:T(8,128)(2,1)S(1)}, bf16[256,2048]{1,0:T(8,128)(2,1)S(1)}, u32[]{:S(2)}, u32[]{:S(2)}) collective-permute-start(bf16[256,2048]{1,0:T(8,128)(2,1)S(1)} %get-tuple-element.31), channel_id=1, source_target_pairs={{0,8},{8,16},{16,24},{1,9},{9,17},{17,25},{2,10},{10,18},{18,26},{... | collective-permute-start | bytes 3145736 | tf_op jit(solution)/shard_map/ppermute | solution.py:315
  218.7 5.7 %late.3 = (f32[448,4096]{1,0:T(8,128)}, bf16[4,448,4096]{2,1,0:T(8,128)(2,1)}, bf16[256,2048]{1,0:T(8,128)(2,1)S(1)}) custom-call(s32[17]{0:T(128)S(1)} %pad_add_fusion.scalars, bf16[4,448,128]{2,1,0:T(8,128)(2,1)S(1)} %bitcast.50, bf16[1024,128]{1,0:T(8,128)(2,1)S(1)} %collective-permute-done.6.refs_1_, ...), custom_call_target="tpu_custom_call", output_to_operand_aliasing={{0}: (10, {}), {1}: (11, {})} | custom-call | flops 536870912 | bytes 7340032 | tf_op jit(solution)/shard_map/late/pallas_call | solution.py:183
  225.7 12.9 %collective-permute-done.27 = bf16[256,2048]{1,0:T(8,128)(2,1)S(1)} collective-permute-done((bf16[256,2048]{1,0:T(8,128)(2,1)S(1)}, bf16[256,2048]{1,0:T(8,128)(2,1)S(1)}, u32[]{:S(2)}, u32[]{:S(2)}) %collective-permute-start.27) | collective-permute-done | bytes 1048608 | tf_op jit(solution)/shard_map/ppermute | solution.py:314
  238.6 1.7 collective-permute-start.22
  240.2 19.2 %residue.1 = bf16[1792,4096]{1,0:T(8,128)(2,1)} custom-call(s32[8]{0:T(128)S(1)} %or_or_fusion.1.slots, bf16[1792,4096]{1,0:T(8,128)(2,1)} %bitcast.56, bf16[1792,4096]{1,0:T(8,128)(2,1)} %bitcast.58, bf16[1792,128]{1,0:T(8,128)(2,1)S(1)} %convolution_convert_fusion.p_ref, bf16[8,256,512]{2,1,0:T(8,128)(2,1)S(1)} %get-tuple-element.32.refs_5_.r_ref), custom_call_target="tpu_custom_call" | custom-call | flops 1879048192 | bytes 44040192 | tf_op jit(solution)/shard_map/residue/pallas_call | solution.py:109
  259.4 1.7 collective-permute-start.29
  261.1 11.1 %collective-permute-done.24.refs_10_ = bf16[192,4096]{1,0:T(8,128)(2,1)S(1)} collective-permute-done((bf16[192,4096]{1,0:T(8,128)(2,1)}, bf16[192,4096]{1,0:T(8,128)(2,1)S(1)}, u32[]{:S(2)}, u32[]{:S(2)}) %collective-permute-start.24) | collective-permute-done | bytes 1572896 | tf_op jit(solution)/shard_map/ppermute | solution.py:307
  274.0 15.7 %early.1 = (f32[448,4096]{1,0:T(8,128)}, bf16[4,448,4096]{2,1,0:T(8,128)(2,1)}) custom-call(s32[17]{0:T(128)} %copy-done.6, bf16[4,448,128]{2,1,0:T(8,128)(2,1)} %bitcast.51, bf16[1024,128]{1,0:T(8,128)(2,1)} %copy-done.2, bf16[1024,128]{1,0:T(8,128)(2,1)} %copy-done.3, bf16[1024,128]{1,0:T(8,128)(2,1)} %copy-done.4, ...), custom_call_target="tpu_custom_call", output_to_operand_aliasing={{0}: (14, {}), {1}: (15, {})} | custom-call | flops 3221225472 | bytes 25165824 | tf_op jit(solution)/shard_map/early/pallas_call | solution.py:249
  289.7 3.8 collective-permute-done.21
  297.6 24.5 %collective-permute-done.31 = bf16[256,2048]{1,0:T(8,128)(2,1)S(1)} collective-permute-done((bf16[256,2048]{1,0:T(8,128)(2,1)S(1)}, bf16[256,2048]{1,0:T(8,128)(2,1)S(1)}, u32[]{:S(2)}, u32[]{:S(2)}) %collective-permute-start.31) | collective-permute-done | bytes 1048608 | tf_op jit(solution)/shard_map/ppermute | solution.py:314
  324.1 20.4 %collective-permute-done.35 = bf16[256,2048]{1,0:T(8,128)(2,1)S(1)} collective-permute-done((bf16[256,2048]{1,0:T(8,128)(2,1)}, bf16[256,2048]{1,0:T(8,128)(2,1)S(1)}, u32[]{:S(2)}, u32[]{:S(2)}) %collective-permute-start.35) | collective-permute-done | bytes 1048608 | tf_op jit(solution)/shard_map/ppermute | solution.py:314
  345.9 1.4 bitcast_dynamic-update-slice_fusion.5
  347.2 2.5 bitcast_dynamic-update-slice_fusion.4
  349.7 17.3 %collective-permute-done.32 = bf16[256,2048]{1,0:T(8,128)(2,1)S(1)} collective-permute-done((bf16[256,2048]{1,0:T(8,128)(2,1)S(1)}, bf16[256,2048]{1,0:T(8,128)(2,1)S(1)}, u32[]{:S(2)}, u32[]{:S(2)}) %collective-permute-start.32) | collective-permute-done | bytes 1048608 | tf_op jit(solution)/shard_map/ppermute | solution.py:314
  368.4 2.5 bitcast_dynamic-update-slice_fusion.2
  370.9 1.4 bitcast_dynamic-update-slice_fusion.1
  372.3 14.4 %collective-permute-done.36 = bf16[256,2048]{1,0:T(8,128)(2,1)S(1)} collective-permute-done((bf16[256,2048]{1,0:T(8,128)(2,1)S(1)}, bf16[256,2048]{1,0:T(8,128)(2,1)S(1)}, u32[]{:S(2)}, u32[]{:S(2)}) %collective-permute-start.36) | collective-permute-done | bytes 1048608 | tf_op jit(solution)/shard_map/ppermute | solution.py:314
  (97 shorter events, 29.3 us)
Async XLA Ops:
  1.6 6.6 %collective-permute-start = (bf16[1,512,128]{2,1,0:T(8,128)(2,1)S(1)}, bf16[1,512,128]{2,1,0:T(8,128)(2,1)S(1)}, u32[]{:S(2)}, u32[]{:S(2)}) collective-permute-start(bf16[1,512,128]{2,1,0:T(8,128)(2,1)S(1)} %convert_element_type.24), channel_id=1, source_target_pairs={{0,4},{1,5},{2,6},{3,7},{4,0},{5,1},{6,2},{7,3},{8,12},{9,13},{10,... | collective-permute-start | bytes 393224 | tf_op jit(solution)/shard_map/ppermute | solution.py:280
  8.2 7.5 %collective-permute-start.1 = (bf16[2,512,128]{2,1,0:T(8,128)(2,1)S(1)}, bf16[2,512,128]{2,1,0:T(8,128)(2,1)S(1)}, u32[]{:S(2)}, u32[]{:S(2)}) collective-permute-start(bf16[2,512,128]{2,1,0:T(8,128)(2,1)S(1)} %pad_maximum_fusion.11), channel_id=1, source_target_pairs={{0,2},{1,3},{2,0},{3,1},{4,6},{5,7},{6,4},{7,5},{8,10},{9,11},{10,... | collective-permute-start | bytes 786440 | tf_op jit(solution)/shard_map/ppermute | solution.py:280
  15.8 2.0 collective-permute-start.2
  33.9 4.5 %collective-permute-start.9 = (f32[4,128,512]{2,1,0:T(8,128)}, f32[4,128,512]{2,1,0:T(8,128)}, u32[]{:S(2)}, u32[]{:S(2)}) collective-permute-start(f32[4,128,512]{2,1,0:T(8,128)} %slice.39), channel_id=1, source_target_pairs={{0,1},{1,0},{2,3},{3,2},{4,5},{5,4},{6,7},{7,6},{8,9},{9,8},{10,11... | collective-permute-start | bytes 3145736 | tf_op jit(solution)/shard_map/ppermute | solution.py:280
  34.1 2.8 collective-permute-start.3
  36.9 4.6 %collective-permute-start.4 = (f32[128,128]{0,1:T(8,128)S(1)}, f32[128,128]{0,1:T(8,128)S(1)}, u32[]{:S(2)}, u32[]{:S(2)}) collective-permute-start(f32[128,128]{0,1:T(8,128)S(1)} %add.109), channel_id=1, source_target_pairs={{0,2},{1,3},{2,0},{3,1},{4,6},{5,7},{6,4},{7,5},{8,10},{9,11},{10,... | collective-permute-start | bytes 196616 | tf_op jit(solution)/shard_map/ppermute | solution.py:280
  39.8 1.0 copy-start.7
  40.8 17.5 %collective-permute-start.10 = (f32[2,128,512]{2,1,0:T(8,128)S(1)}, f32[2,128,512]{2,1,0:T(8,128)S(1)}, u32[]{:S(2)}, u32[]{:S(2)}) collective-permute-start(f32[2,128,512]{2,1,0:T(8,128)S(1)} %slice.47), channel_id=1, source_target_pairs={{0,2},{1,3},{2,0},{3,1},{4,6},{5,7},{6,4},{7,5},{8,10},{9,11},{10,... | collective-permute-start | bytes 1572872 | tf_op jit(solution)/shard_map/ppermute | solution.py:280
  41.5 4.3 %collective-permute-start.5 = (f32[128,128]{0,1:T(8,128)S(1)}, f32[128,128]{0,1:T(8,128)S(1)}, u32[]{:S(2)}, u32[]{:S(2)}) collective-permute-start(f32[128,128]{0,1:T(8,128)S(1)} %add.110), channel_id=1, source_target_pairs={{0,4},{1,5},{2,6},{3,7},{4,0},{5,1},{6,2},{7,3},{8,12},{9,13},{10,... | collective-permute-start | bytes 196616 | tf_op jit(solution)/shard_map/ppermute | solution.py:280
  59.6 12.2 %collective-permute-start.11 = (f32[1,128,512]{2,1,0:T(8,128)S(1)}, f32[1,128,512]{2,1,0:T(8,128)S(1)}, u32[]{:S(2)}, u32[]{:S(2)}) collective-permute-start(f32[1,128,512]{2,1,0:T(8,128)S(1)} %slice.49), channel_id=1, source_target_pairs={{0,4},{1,5},{2,6},{3,7},{4,0},{5,1},{6,2},{7,3},{8,12},{9,13},{10,... | collective-permute-start | bytes 786440 | tf_op jit(solution)/shard_map/ppermute | solution.py:280
  72.2 7.5 %collective-permute-start.12 = (bf16[1,128,512]{2,1,0:T(8,128)(2,1)S(1)}, bf16[1,128,512]{2,1,0:T(8,128)(2,1)S(1)}, u32[]{:S(2)}, u32[]{:S(2)}) collective-permute-start(bf16[1,128,512]{2,1,0:T(8,128)(2,1)S(1)} %fusion), channel_id=1, source_target_pairs={{0,24},{8,0},{16,8},{24,16},{1,25},{9,1},{17,9},{25,17},{2,26},{10... | collective-permute-start | bytes 393224 | tf_op jit(solution)/shard_map/ppermute | solution.py:299
  75.8 9.0 %collective-permute-start.16 = (bf16[1,128,512]{2,1,0:T(8,128)(2,1)S(1)}, bf16[1,128,512]{2,1,0:T(8,128)(2,1)S(1)}, u32[]{:S(2)}, u32[]{:S(2)}) collective-permute-start(bf16[1,128,512]{2,1,0:T(8,128)(2,1)S(1)} %fusion), channel_id=1, source_target_pairs={{0,16},{8,24},{16,0},{24,8},{1,17},{9,25},{17,1},{25,9},{2,18},{10... | collective-permute-start | bytes 393224 | tf_op jit(solution)/shard_map/ppermute | solution.py:299
  79.7 9.3 %collective-permute-start.13 = (bf16[1,256,512]{2,1,0:T(8,128)(2,1)S(1)}, bf16[1,256,512]{2,1,0:T(8,128)(2,1)S(1)}, u32[]{:S(2)}, u32[]{:S(2)}) collective-permute-start(bf16[1,256,512]{2,1,0:T(8,128)(2,1)S(1)} %pad_maximum_fusion.12), channel_id=1, source_target_pairs={{0,4},{1,5},{2,6},{3,7},{4,0},{5,1},{6,2},{7,3},{8,12},{9,13},{10,... | collective-permute-start | bytes 786440 | tf_op jit(solution)/shard_map/ppermute | solution.py:280
  79.9 7.2 %collective-permute-start.17 = (bf16[1,128,512]{2,1,0:T(8,128)(2,1)S(1)}, bf16[1,128,512]{2,1,0:T(8,128)(2,1)S(1)}, u32[]{:S(2)}, u32[]{:S(2)}) collective-permute-start(bf16[1,128,512]{2,1,0:T(8,128)(2,1)S(1)} %fusion), channel_id=1, source_target_pairs={{0,8},{8,16},{16,24},{24,0},{1,9},{9,17},{17,25},{25,1},{2,10},{10... | collective-permute-start | bytes 393224 | tf_op jit(solution)/shard_map/ppermute | solution.py:299
  87.1 9.2 %collective-permute-start.18 = (bf16[1,256,512]{2,1,0:T(8,128)(2,1)S(1)}, bf16[1,256,512]{2,1,0:T(8,128)(2,1)S(1)}, u32[]{:S(2)}, u32[]{:S(2)}) collective-permute-start(bf16[1,256,512]{2,1,0:T(8,128)(2,1)S(1)} %constant_dynamic-update-slice_fusion), channel_id=1, source_target_pairs={{0,2},{1,3},{2,0},{3,1},{4,6},{5,7},{6,4},{7,5},{8,10},{9,11},{10,... | collective-permute-start | bytes 786440 | tf_op jit(solution)/shard_map/ppermute | solution.py:280
  89.0 14.1 %collective-permute-start.14 = (bf16[2,256,512]{2,1,0:T(8,128)(2,1)S(1)}, bf16[2,256,512]{2,1,0:T(8,128)(2,1)S(1)}, u32[]{:S(2)}, u32[]{:S(2)}) collective-permute-start(bf16[2,256,512]{2,1,0:T(8,128)(2,1)S(1)} %pad_maximum_fusion.6), channel_id=1, source_target_pairs={{0,2},{1,3},{2,0},{3,1},{4,6},{5,7},{6,4},{7,5},{8,10},{9,11},{10,... | collective-permute-start | bytes 1572872 | tf_op jit(solution)/shard_map/ppermute | solution.py:280
  96.4 9.2 %collective-permute-start.19 = (bf16[2,256,512]{2,1,0:T(8,128)(2,1)S(1)}, bf16[2,256,512]{2,1,0:T(8,128)(2,1)S(1)}, u32[]{:S(2)}, u32[]{:S(2)}) collective-permute-start(bf16[2,256,512]{2,1,0:T(8,128)(2,1)S(1)} %pad_maximum_fusion.7), channel_id=1, source_target_pairs={{0,4},{1,5},{2,6},{3,7},{4,0},{5,1},{6,2},{7,3},{8,12},{9,13},{10,... | collective-permute-start | bytes 1572872 | tf_op jit(solution)/shard_map/ppermute | solution.py:280
  104.2 12.8 %collective-permute-start.15 = (bf16[4,256,512]{2,1,0:T(8,128)(2,1)}, bf16[4,256,512]{2,1,0:T(8,128)(2,1)}, u32[]{:S(2)}, u32[]{:S(2)}) collective-permute-start(bf16[4,256,512]{2,1,0:T(8,128)(2,1)} %pad_maximum_fusion.3), channel_id=1, source_target_pairs={{0,1},{1,0},{2,3},{3,2},{4,5},{5,4},{6,7},{7,6},{8,9},{9,8},{10,11... | collective-permute-start | bytes 3145736 | tf_op jit(solution)/shard_map/ppermute | solution.py:280
  106.8 12.1 %collective-permute-start.20 = (bf16[4,256,512]{2,1,0:T(8,128)(2,1)}, bf16[4,256,512]{2,1,0:T(8,128)(2,1)}, u32[]{:S(2)}, u32[]{:S(2)}) collective-permute-start(bf16[4,256,512]{2,1,0:T(8,128)(2,1)} %pad_maximum_fusion.4), channel_id=1, source_target_pairs={{0,1},{1,0},{2,3},{3,2},{4,5},{5,4},{6,7},{7,6},{8,9},{9,8},{10,11... | collective-permute-start | bytes 3145736 | tf_op jit(solution)/shard_map/ppermute | solution.py:280
  110.0 106.6 %collective-permute-start.23 = (bf16[192,4096]{1,0:T(8,128)(2,1)}, bf16[192,4096]{1,0:T(8,128)(2,1)}, u32[]{:S(2)}, u32[]{:S(2)}) collective-permute-start(bf16[192,4096]{1,0:T(8,128)(2,1)} %slice.58), channel_id=1, source_target_pairs={{0,24},{8,0},{16,8},{24,16},{1,25},{9,1},{17,9},{25,17},{2,26},{10... | collective-permute-start | bytes 4718600 | tf_op jit(solution)/shard_map/ppermute | solution.py:299
  112.0 105.8 %collective-permute-start.25 = (bf16[192,4096]{1,0:T(8,128)(2,1)}, bf16[192,4096]{1,0:T(8,128)(2,1)}, u32[]{:S(2)}, u32[]{:S(2)}) collective-permute-start(bf16[192,4096]{1,0:T(8,128)(2,1)} %slice.58), channel_id=1, source_target_pairs={{0,8},{8,16},{16,24},{24,0},{1,9},{9,17},{17,25},{25,1},{2,10},{10... | collective-permute-start | bytes 4718600 | tf_op jit(solution)/shard_map/ppermute | solution.py:299
  112.4 106.2 %copy-start.6 = (s32[17]{0:T(128)}, s32[17]{0:T(128)S(1)}, u32[]{:S(2)}) copy-start(s32[17]{0:T(128)S(1)} %pad_add_fusion.scalars) | copy-start | bytes 208
  113.3 126.9 %copy-start.1 = (bf16[1792,128]{1,0:T(8,128)(2,1)}, bf16[1792,128]{1,0:T(8,128)(2,1)S(1)}, u32[]{:S(2)}) copy-start(bf16[1792,128]{1,0:T(8,128)(2,1)S(1)} %convolution_convert_fusion.p_ref) | copy-start | bytes 1376260
  113.4 73.5 %collective-permute-start.6 = (bf16[1024,128]{1,0:T(8,128)(2,1)S(1)}, bf16[1024,128]{1,0:T(8,128)(2,1)S(1)}, u32[]{:S(2)}, u32[]{:S(2)}) collective-permute-start(bf16[1024,128]{1,0:T(8,128)(2,1)S(1)} %get-tuple-element.48), channel_id=1, source_target_pairs={{0,24},{8,0},{16,8},{24,16},{1,25},{9,1},{17,9},{25,17},{2,26},{10... | collective-permute-start | bytes 786440 | tf_op jit(solution)/shard_map/ppermute | solution.py:299
  117.0 88.0 %collective-permute-start.7 = (bf16[1024,128]{1,0:T(8,128)(2,1)S(1)}, bf16[1024,128]{1,0:T(8,128)(2,1)S(1)}, u32[]{:S(2)}, u32[]{:S(2)}) collective-permute-start(bf16[1024,128]{1,0:T(8,128)(2,1)S(1)} %get-tuple-element.47), channel_id=1, source_target_pairs={{0,16},{8,24},{16,0},{24,8},{1,17},{9,25},{17,1},{25,9},{2,18},{10... | collective-permute-start | bytes 786440 | tf_op jit(solution)/shard_map/ppermute | solution.py:299
  118.9 121.4 %copy-start = (bf16[8,256,512]{2,1,0:T(8,128)(2,1)}, bf16[8,256,512]{2,1,0:T(8,128)(2,1)S(1)}, u32[]{:S(2)}) copy-start(bf16[8,256,512]{2,1,0:T(8,128)(2,1)S(1)} %get-tuple-element.32.refs_5_.r_ref) | copy-start | bytes 6291460
  118.9 86.1 %collective-permute-start.8 = (bf16[1024,128]{1,0:T(8,128)(2,1)S(1)}, bf16[1024,128]{1,0:T(8,128)(2,1)S(1)}, u32[]{:S(2)}, u32[]{:S(2)}) collective-permute-start(bf16[1024,128]{1,0:T(8,128)(2,1)S(1)} %get-tuple-element.46), channel_id=1, source_target_pairs={{0,8},{8,16},{16,24},{24,0},{1,9},{9,17},{17,25},{25,1},{2,10},{10... | collective-permute-start | bytes 786440 | tf_op jit(solution)/shard_map/ppermute | solution.py:299
  122.8 95.9 %copy-start.5 = (f32[1,512]{1,0:T(1,128)}, f32[1,512]{1,0:T(1,128)S(1)}, u32[]{:S(2)}) copy-start(f32[1,512]{1,0:T(1,128)S(1)} %fusion.8.refs_4_) | copy-start | bytes 6148
  186.9 31.7 %copy-start.2 = (bf16[1024,128]{1,0:T(8,128)(2,1)}, bf16[1024,128]{1,0:T(8,128)(2,1)S(1)}, u32[]{:S(2)}) copy-start(bf16[1024,128]{1,0:T(8,128)(2,1)S(1)} %collective-permute-done.6.refs_1_) | copy-start | bytes 786436
  205.0 13.7 %copy-start.3 = (bf16[1024,128]{1,0:T(8,128)(2,1)}, bf16[1024,128]{1,0:T(8,128)(2,1)S(1)}, u32[]{:S(2)}) copy-start(bf16[1024,128]{1,0:T(8,128)(2,1)S(1)} %collective-permute-done.7.refs_2_) | copy-start | bytes 786436
  205.0 13.7 %copy-start.4 = (bf16[1024,128]{1,0:T(8,128)(2,1)}, bf16[1024,128]{1,0:T(8,128)(2,1)S(1)}, u32[]{:S(2)}) copy-start(bf16[1024,128]{1,0:T(8,128)(2,1)S(1)} %collective-permute-done.8.refs_3_) | copy-start | bytes 786436
  210.6 27.9 %collective-permute-start.27 = (bf16[256,2048]{1,0:T(8,128)(2,1)S(1)}, bf16[256,2048]{1,0:T(8,128)(2,1)S(1)}, u32[]{:S(2)}, u32[]{:S(2)}) collective-permute-start(bf16[256,2048]{1,0:T(8,128)(2,1)S(1)} %get-tuple-element.31), channel_id=1, source_target_pairs={{8,0},{16,8},{24,16},{9,1},{17,9},{25,17},{10,2},{18,10},{26,18},{... | collective-permute-start | bytes 3145736 | tf_op jit(solution)/shard_map/ppermute | solution.py:314
  211.9 47.5 %collective-permute-start.28 = (bf16[256,2048]{1,0:T(8,128)(2,1)S(1)}, bf16[256,2048]{1,0:T(8,128)(2,1)S(1)}, u32[]{:S(2)}, u32[]{:S(2)}) collective-permute-start(bf16[256,2048]{1,0:T(8,128)(2,1)S(1)} %get-tuple-element.31), channel_id=1, source_target_pairs={{0,8},{8,16},{16,24},{1,9},{9,17},{17,25},{2,10},{10,18},{18,26},{... | collective-permute-start | bytes 3145736 | tf_op jit(solution)/shard_map/ppermute | solution.py:315
  216.6 55.7 %collective-permute-start.24 = (bf16[192,4096]{1,0:T(8,128)(2,1)}, bf16[192,4096]{1,0:T(8,128)(2,1)S(1)}, u32[]{:S(2)}, u32[]{:S(2)}) collective-permute-start(bf16[192,4096]{1,0:T(8,128)(2,1)} %collective-permute-done.23.refs_9_), channel_id=1, source_target_pairs={{8,0},{16,8},{9,1},{17,9},{10,2},{18,10},{11,3},{19,11},{12,4},{20... | collective-permute-start | bytes 4718600 | tf_op jit(solution)/shard_map/ppermute | solution.py:307
  217.9 54.4 %collective-permute-start.26 = (bf16[192,4096]{1,0:T(8,128)(2,1)}, bf16[192,4096]{1,0:T(8,128)(2,1)S(1)}, u32[]{:S(2)}, u32[]{:S(2)}) collective-permute-start(bf16[192,4096]{1,0:T(8,128)(2,1)} %collective-permute-done.25.refs_12_), channel_id=1, source_target_pairs={{8,16},{16,24},{9,17},{17,25},{10,18},{18,26},{11,19},{19,27},{12,... | collective-permute-start | bytes 4718600 | tf_op jit(solution)/shard_map/ppermute | solution.py:308
  224.4 69.2 %collective-permute-start.21 = (bf16[256,2048]{1,0:T(8,128)(2,1)S(1)}, bf16[256,2048]{1,0:T(8,128)(2,1)}, u32[]{:S(2)}, u32[]{:S(2)}) collective-permute-start(bf16[256,2048]{1,0:T(8,128)(2,1)S(1)} %get-tuple-element.26), channel_id=1, source_target_pairs={{8,0},{16,8},{24,16},{9,1},{17,9},{25,17},{10,2},{18,10},{26,18},{... | collective-permute-start | bytes 3145736 | tf_op jit(solution)/shard_map/ppermute | solution.py:314
  238.6 55.0 %collective-permute-start.22 = (bf16[256,2048]{1,0:T(8,128)(2,1)S(1)}, bf16[256,2048]{1,0:T(8,128)(2,1)S(1)}, u32[]{:S(2)}, u32[]{:S(2)}) collective-permute-start(bf16[256,2048]{1,0:T(8,128)(2,1)S(1)} %get-tuple-element.26), channel_id=1, source_target_pairs={{0,8},{8,16},{16,24},{1,9},{9,17},{17,25},{2,10},{10,18},{18,26},{... | collective-permute-start | bytes 3145736 | tf_op jit(solution)/shard_map/ppermute | solution.py:315
  259.4 37.4 %collective-permute-start.29 = (bf16[256,2048]{1,0:T(8,128)(2,1)S(1)}, bf16[256,2048]{1,0:T(8,128)(2,1)}, u32[]{:S(2)}, u32[]{:S(2)}) collective-permute-start(bf16[256,2048]{1,0:T(8,128)(2,1)S(1)} %collective-permute-done.28), channel_id=1, source_target_pairs={{8,16},{16,24},{9,17},{17,25},{10,18},{18,26},{11,19},{19,27},{12,... | collective-permute-start | bytes 3145736 | tf_op jit(solution)/shard_map/ppermute | solution.py:315
  272.3 1.2 copy-start.8
  272.3 1.8 copy-start.9
  293.5 28.6 %collective-permute-start.31 = (bf16[256,2048]{1,0:T(8,128)(2,1)S(1)}, bf16[256,2048]{1,0:T(8,128)(2,1)S(1)}, u32[]{:S(2)}, u32[]{:S(2)}) collective-permute-start(bf16[256,2048]{1,0:T(8,128)(2,1)S(1)} %collective-permute-done.27), channel_id=1, source_target_pairs={{8,0},{16,8},{9,1},{17,9},{10,2},{18,10},{11,3},{19,11},{12,4},{20... | collective-permute-start | bytes 3145736 | tf_op jit(solution)/shard_map/ppermute | solution.py:314
  294.8 28.6 %collective-permute-start.33 = (bf16[256,2048]{1,0:T(8,128)(2,1)S(1)}, bf16[256,2048]{1,0:T(8,128)(2,1)S(1)}, u32[]{:S(2)}, u32[]{:S(2)}) collective-permute-start(bf16[256,2048]{1,0:T(8,128)(2,1)S(1)} %collective-permute-done.22), channel_id=1, source_target_pairs={{8,16},{16,24},{9,17},{17,25},{10,18},{18,26},{11,19},{19,27},{12,... | collective-permute-start | bytes 3145736 | tf_op jit(solution)/shard_map/ppermute | solution.py:315
  295.6 49.0 %collective-permute-start.35 = (bf16[256,2048]{1,0:T(8,128)(2,1)}, bf16[256,2048]{1,0:T(8,128)(2,1)S(1)}, u32[]{:S(2)}, u32[]{:S(2)}) collective-permute-start(bf16[256,2048]{1,0:T(8,128)(2,1)} %collective-permute-done.21), channel_id=1, source_target_pairs={{8,0},{16,8},{9,1},{17,9},{10,2},{18,10},{11,3},{19,11},{12,4},{20... | collective-permute-start | bytes 3145736 | tf_op jit(solution)/shard_map/ppermute | solution.py:314
  296.9 49.0 %collective-permute-start.30 = (bf16[256,2048]{1,0:T(8,128)(2,1)}, bf16[256,2048]{1,0:T(8,128)(2,1)S(1)}, u32[]{:S(2)}, u32[]{:S(2)}) collective-permute-start(bf16[256,2048]{1,0:T(8,128)(2,1)} %collective-permute-done.29), channel_id=1, source_target_pairs={{16,24},{17,25},{18,26},{19,27},{20,28},{21,29},{22,30},{23,31}} | collective-permute-start | bytes 3145736 | tf_op jit(solution)/shard_map/ppermute | solution.py:315
  322.1 44.9 %collective-permute-start.32 = (bf16[256,2048]{1,0:T(8,128)(2,1)S(1)}, bf16[256,2048]{1,0:T(8,128)(2,1)S(1)}, u32[]{:S(2)}, u32[]{:S(2)}) collective-permute-start(bf16[256,2048]{1,0:T(8,128)(2,1)S(1)} %collective-permute-done.31), channel_id=1, source_target_pairs={{8,0},{9,1},{10,2},{11,3},{12,4},{13,5},{14,6},{15,7}} | collective-permute-start | bytes 3145736 | tf_op jit(solution)/shard_map/ppermute | solution.py:314
  323.4 45.0 %collective-permute-start.34 = (bf16[256,2048]{1,0:T(8,128)(2,1)S(1)}, bf16[256,2048]{1,0:T(8,128)(2,1)S(1)}, u32[]{:S(2)}, u32[]{:S(2)}) collective-permute-start(bf16[256,2048]{1,0:T(8,128)(2,1)S(1)} %collective-permute-done.33), channel_id=1, source_target_pairs={{16,24},{17,25},{18,26},{19,27},{20,28},{21,29},{22,30},{23,31}} | collective-permute-start | bytes 3145736 | tf_op jit(solution)/shard_map/ppermute | solution.py:315
  344.6 42.1 %collective-permute-start.36 = (bf16[256,2048]{1,0:T(8,128)(2,1)S(1)}, bf16[256,2048]{1,0:T(8,128)(2,1)S(1)}, u32[]{:S(2)}, u32[]{:S(2)}) collective-permute-start(bf16[256,2048]{1,0:T(8,128)(2,1)S(1)} %collective-permute-done.35), channel_id=1, source_target_pairs={{8,0},{9,1},{10,2},{11,3},{12,4},{13,5},{14,6},{15,7}} | collective-permute-start | bytes 3145736 | tf_op jit(solution)/shard_map/ppermute | solution.py:314
